TPU v7x, 128 devices: a whole 4x4x4 slice. The times are simulated.
128 devices in a mesh: section: 2 (over x_hi), expert: 16 (over z, y), tensor: 4 (over x_lo, core).
Axes of the slice: x: 4 (x_hi: 2, x_lo: 2; x = x_hi * 2 + x_lo), y: 4, z: 4, core: 2. Of those that a mesh axis runs over, the one named last changes fastest.
Arguments:
- layer_inputs: bfloat16 [2, 2, 1280, 3072], P('section', None, 'expert', 'tensor'), may hold values from -6 to 6
- grad_out: bfloat16 [2, 1280, 3072], P(None, 'expert', 'tensor'), may hold values from -6 to 6
- norm_gain: bfloat16 [2, 3072], P('section', 'tensor'), may hold values from 0.25 to 1.75
- router_w: bfloat16 [2, 3072, 4], P('section', 'tensor'), may hold values from -0.21875 to 0.21875
- w_gate: bfloat16 [2, 3072, 32768], P('section', None, ('expert', 'tensor')), may hold values from -0.109375 to 0.109375
- w_up: bfloat16 [2, 3072, 32768], P('section', None, ('expert', 'tensor')), may hold values from -0.109375 to 0.109375
- w_down: bfloat16 [2, 32768, 3072], P('section', ('expert', 'tensor')), may hold values from -0.0625 to 0.0625
- saved_gate: bfloat16 [2, 2, 16, 64, 32768], P('section', None, None, None, ('expert', 'tensor')), may hold values from -6 to 6
- saved_up: bfloat16 [2, 2, 16, 64, 32768], P('section', None, None, None, ('expert', 'tensor')), may hold values from -6 to 6
- routes: int32 [2, 2, 1280, 2], P('section', None, 'expert'), may hold values from 0 to 3, all different within a row; in each aligned block of 80 rows (0 to 79, 80 to 159, ..., all dimensions but the last counted through in order) at most 64 rows name the same one
Outputs:
- layer_grads: bfloat16 [2, 2, 1280, 3072], P('section', None, 'expert', 'tensor')
Inputs may be any that keep to these rules, and one draw needn't show every extreme that they name: `routes`: each token names two different experts; within the 80 tokens of one device's aligned block of a layer and micro-batch, no expert is named by more than 64 tokens, and in some blocks one expert is named by exactly 64.
All inputs are finite; a program needn't handle non-finite values.
Results may differ from a plain program's by a relative error of at most 0.011.
Values may be sent and summed in bfloat16 or wider, within the bound.
A program may use at most 128 MiB of HBM per device.

v0:
```python
import jax
import jax.numpy as jnp
from jax import lax
from jax.sharding import PartitionSpec as P

norm_eps = 1e-05
highest = lax.Precision.HIGHEST


def from_everyone(value, axis):
    copies = jnp.broadcast_to(value, (lax.axis_size(axis), *value.shape))
    return lax.all_to_all(copies, axis, split_axis=0, concat_axis=0, tiled=True)


def taken_together(value, axis):
    return from_everyone(value, axis).sum(axis=0)


def from_behind(block, axis, distance):
    devices = range(lax.axis_size(axis))
    route = [(i - distance, i) for i in devices if i - distance in devices]
    return lax.ppermute(block, axis, route)


def on_device(
    layer_inputs, grad_out, norm_gain, router_w, w_gate, w_up, w_down, saved_gate, saved_up, routes
):
    sections = lax.axis_size("section")
    position = lax.axis_index("section")
    holders = lax.axis_size("expert")
    micros = grad_out.shape[0]
    tokens_here = grad_out.shape[1]
    quarter = grad_out.shape[2]
    gain_full = norm_gain[0].astype(jnp.float32)
    router = router_w[0]
    gate_mat = w_gate[0]
    up_mat = w_up[0]
    down_mat = w_down[0]
    width_all = gate_mat.shape[0]
    experts = router.shape[1]
    group = holders // experts
    capacity = saved_gate.shape[3]
    slot_count = experts * capacity
    slot_ids = jnp.arange(slot_count, dtype=jnp.int32)
    expert_ids = jnp.arange(experts, dtype=jnp.int32)

    def add_columns(piece):
        return jnp.einsum("scw,fw->scf", piece, down_mat, preferred_element_type=jnp.float32)

    def layer_back(inputs, upstream, chosen, gate_saved, up_saved):
        values = inputs.astype(jnp.float32)
        squares = taken_together(jnp.sum(values * values, axis=-1), "tensor")
        scale = lax.rsqrt(squares / width_all + norm_eps)[:, None]
        normed = (values * scale * gain_full).astype(jnp.bfloat16)
        partial_logits = jnp.dot(normed, router, preferred_element_type=jnp.float32)
        logits = lax.psum(partial_logits, "tensor")
        onehot = (chosen[:, :, None] == expert_ids[None, None, :]).astype(jnp.float32)
        picked = jnp.sum(onehot * logits[:, None, :], axis=-1)
        first = jax.nn.sigmoid(picked[:, 0] - picked[:, 1])
        second = jax.nn.sigmoid(picked[:, 1] - picked[:, 0])
        flat_hot = onehot.reshape(tokens_here * 2, experts)
        earlier = jnp.cumsum(flat_hot, axis=0) - flat_hot
        within = jnp.sum(earlier * flat_hot, axis=-1).astype(jnp.int32)
        target = chosen.reshape(tokens_here * 2) * capacity + within
        placing = (
            (slot_ids[:, None] == target[None, :])
            .astype(jnp.float32)
            .reshape(slot_count, tokens_here, 2)
        )
        select = jnp.sum(placing, axis=-1).astype(jnp.bfloat16)
        upstream_send = jnp.dot(select, upstream, preferred_element_type=jnp.float32).astype(
            jnp.bfloat16
        )
        copies = jnp.broadcast_to(
            upstream_send.reshape(experts, 1, capacity, quarter),
            (experts, group, capacity, quarter),
        ).reshape(holders, capacity, quarter)
        arrived = lax.all_to_all(copies, "expert", split_axis=0, concat_axis=0, tiled=True)
        back_act = add_columns(lax.all_gather(arrived, "tensor", axis=2, tiled=True))
        gate_act = gate_saved.astype(jnp.float32)
        up_act = up_saved.astype(jnp.float32)
        sigma = jax.nn.sigmoid(gate_act)
        swish = gate_act * sigma
        weight_part = jnp.sum(swish * up_act * back_act, axis=-1)
        slope = sigma * (1.0 + gate_act * (1.0 - sigma))
        gate_grad = (back_act * up_act * slope).astype(jnp.bfloat16)
        up_grad = (back_act * swish).astype(jnp.bfloat16)
        unit = jnp.einsum("scf,df->scd", gate_grad, gate_mat, preferred_element_type=jnp.float32)
        unit = unit + jnp.einsum("scf,df->scd", up_grad, up_mat, preferred_element_type=jnp.float32)
        weighted = placing[:, :, 0] * first[None, :] + placing[:, :, 1] * second[None, :]
        unit_share = lax.psum_scatter(
            unit.astype(jnp.bfloat16), "tensor", scatter_dimension=2, tiled=True
        ).astype(jnp.float32)
        back_units, back_weights = (
            lax.all_to_all(unit_share, "expert", split_axis=0, concat_axis=0, tiled=True),
            lax.all_to_all(weight_part, "expert", split_axis=0, concat_axis=0, tiled=True),
        )
        slot_units = jnp.sum(back_units.reshape(experts, group, capacity, quarter), axis=1).reshape(
            slot_count, quarter
        )
        slot_weight = jnp.sum(back_weights.reshape(experts, group, capacity), axis=1).reshape(
            slot_count
        )
        hidden_grad = lax.dot_general(
            weighted, slot_units, (((0,), (0,)), ((), ())), precision=highest
        )
        prob_part = jnp.einsum("stk,s->tk", placing, slot_weight, precision=highest)
        prob_grad = taken_together(prob_part, "tensor")
        logit_step = first * second * (prob_grad[:, 0] - prob_grad[:, 1])
        logit_grad = (onehot[:, 0, :] - onehot[:, 1, :]) * logit_step[:, None]
        hidden_grad = hidden_grad + jnp.einsum(
            "te,de->td", logit_grad, router.astype(jnp.float32), precision=highest
        )
        gained = hidden_grad * gain_full
        moment = lax.psum(jnp.sum(values * gained, axis=-1), "tensor")[:, None] / width_all
        result = (
            upstream.astype(jnp.float32) + scale * gained - values * scale * scale * scale * moment
        )
        return result.astype(jnp.bfloat16)

    def advance(tick, carry):
        incoming, grads = carry
        micro_id = tick - (sections - 1 - position)
        valid = jnp.logical_and(micro_id >= 0, micro_id < micros)
        safe_id = jnp.clip(micro_id, 0, micros - 1)
        inputs = lax.dynamic_index_in_dim(layer_inputs[0], safe_id, 0, keepdims=False)
        top_grad = lax.dynamic_index_in_dim(grad_out, safe_id, 0, keepdims=False)
        chosen = lax.dynamic_index_in_dim(routes[0], safe_id, 0, keepdims=False)
        gate_saved = lax.dynamic_index_in_dim(saved_gate[0], safe_id, 0, keepdims=False)
        up_saved = lax.dynamic_index_in_dim(saved_up[0], safe_id, 0, keepdims=False)
        upstream = jnp.where(position == sections - 1, top_grad, incoming)
        computed = layer_back(inputs, upstream, chosen, gate_saved, up_saved)
        result = jnp.where(valid, computed, jnp.zeros_like(computed))
        updated = lax.dynamic_update_index_in_dim(grads, result, safe_id, 0)
        grads = jnp.where(valid, updated, grads)
        incoming = from_behind(result, "section", -1)
        return (incoming, grads)

    start = (
        jnp.zeros((tokens_here, quarter), jnp.bfloat16),
        jnp.zeros((micros, tokens_here, quarter), jnp.bfloat16),
    )
    final_in, grads = lax.fori_loop(0, micros + sections - 1, advance, start)
    return grads[None]


def solution(mesh):
    placed = (
        P("section", None, "expert", "tensor"),
        P(None, "expert", "tensor"),
        P("section", "tensor"),
        P("section", "tensor", None),
        P("section", None, ("expert", "tensor")),
        P("section", None, ("expert", "tensor")),
        P("section", ("expert", "tensor"), None),
        P("section", None, None, None, ("expert", "tensor")),
        P("section", None, None, None, ("expert", "tensor")),
        P("section", None, "expert", None),
    )
    return jax.shard_map(
        on_device,
        mesh=mesh,
        in_specs=placed,
        out_specs=P("section", None, "expert", "tensor"),
        check_vma=False,
    )
```

profile of v0, /device:TPU:1, one launch (start us, length us, event | category | flops | bytes accessed | tf_op | source)
XLA Modules:
  0.0 786.6 jit_solution(16155835591769332147)
XLA Ops:
  8.0 771.7 %while.19 = (s32[]{:T(128)}, bf16[80,768]{1,0:T(8,128)(2,1)S(1)}, bf16[2,80,768]{2,1,0:T(8,128)(2,1)}, s32[]{:T(128)}, pred[]{:T(512)}, /*index=5*/bf16[2,80,768...) while((s32[]{:T(128)}, bf16[80,768]{1,0:T(8,128)(2,1)S(1)}, ...), condition=%wide.region_16.17_spmd.clone.clone, body=%wide.region_0.16_spmd.clone.clone.sunk | while | flops 9912379392 | bytes 199243984 | solution.py:143
  9.0 1.2 reduce-window.24
  11.7 1.2 convolution_convert_fusion.2
  13.0 30.4 %all_to_all.76 = bf16[16,64,768]{2,1,0:T(8,128)(2,1)} all-to-all(bf16[16,64,768]{2,1,0:T(8,128)(2,1)S(1)} %bitcast.176), channel_id=1, replica_groups=mesh['section'=2,'expert'=16,'tensor'=4] {'expert'}, dimensions={0} | all-to-all | bytes 3145728 | tf_op jit(solution)/shard_map/while/body/eval_jaxpr/all_to_all | solution.py:78
  43.5 63.3 %all-gather.2.cloned.1.call-done = bf16[16,64,3072]{2,1,0:T(8,128)(2,1)} async-done(((bf16[16,64,768]{2,1,0:T(8,128)(2,1)}), bf16[16,64,3072]{2,1,0:T(8,128)(2,1)}) %all-gather.2.cloned.1.call-update) | async-done | bytes 6291472 | tf_op jit(solution)/shard_map/while/body/eval_jaxpr/all_gather | solution.py:79
  106.8 8.0 %fusion.118 = (f32[16,64]{1,0:T(8,128)}, f32[16,64,512]{2,1,0:T(8,128)S(1)}) fusion(bf16[1,2,16,64,512]{4,3,2,1,0:T(8,128)(2,1)} %get-tuple-element.705, s32[]{:T(128)S(6)} %min.13, bf16[1,2,16,64,512]{4,3,2,1,0:T(8,128)(2,1)} %get-tuple-element.706, bf16[16,64,3072]{2,1,0:T(8,128)(2,1)} %all-gather.2.cloned.1.call-done, ...), kind=kOutput, calls=%fused_computation.17.clone.1 | convolution fusion | flops 3225943040 | bytes 13635588 | tf_op jit(solution)/shard_map/while/body/eval_jaxpr/scw,fw->scf/dot_general | solution.py:48
  114.8 7.1 fusion.124
  122.0 9.1 %add_convert_fusion.2 = bf16[16,64,3072]{2,1,0:T(8,128)(2,1)} fusion(f32[16,64,3072]{2,1,0:T(8,128)} %fusion.124, bf16[3072,512]{1,0:T(8,128)(2,1)S(1)} %copy-done.7, f32[16,64,512]{2,1,0:T(8,128)} %copy-done.10, bf16[1,2,16,64,512]{4,3,2,1,0:T(8,128)(2,1)S(1)} %copy-done.9, s32[]{:T(128)S(6)} %min.13), kind=kOutput, calls=%fused_computation.2.clone.1 | convolution fusion | flops 3231186944 | bytes 25165828 | tf_op jit(solution)/shard_map/while/body/eval_jaxpr/scf,df->scd/dot_general | solution.py:89
  131.1 6.8 all-to-all-start.1
  138.1 6.3 all-to-all-done.1
  145.0 3.7 all-to-all-start.3
  149.0 3.3 all-to-all-done.3
  152.9 3.5 all-to-all-start.2
  156.4 38.1 %reduce-scatter.2.cloned.1.call-done = bf16[16,64,768]{2,1,0:T(8,128)(2,1)} async-done(((bf16[16,64,3072]{2,1,0:T(8,128)(2,1)}), bf16[16,64,768]{2,1,0:T(8,128)(2,1)}) %reduce-scatter.2.cloned.1.call-update) | async-done | bytes 1572880 | tf_op jit(solution)/shard_map/while/body/eval_jaxpr/reduce_scatter | solution.py:91
  194.5 3.4 convert_element_type.262
  197.9 6.8 all-to-all-start.4
  205.8 5.7 psum.32
  211.8 40.5 %all-to-all-done.4 = f32[16,64,768]{2,1,0:T(8,128)S(1)} async-done(((f32[16,64,768]{2,1,0:T(8,128)}), f32[16,64,768]{2,1,0:T(8,128)S(1)}, u32[]{:S(2)}, u32[]{:S(2)}) %all-to-all-start.4) | async-done | bytes 3145760 | tf_op jit(solution)/shard_map/while/body/eval_jaxpr/all_to_all | solution.py:95
  254.1 6.5 psum.33
  260.6 1.8 fusion.127
  262.5 1.3 collective-permute-start
  263.8 5.8 collective-permute-done
  270.5 1.2 reduce-window.24
  273.2 1.2 convolution_convert_fusion.2
  274.6 25.6 %all_to_all.76 = bf16[16,64,768]{2,1,0:T(8,128)(2,1)} all-to-all(bf16[16,64,768]{2,1,0:T(8,128)(2,1)S(1)} %bitcast.176), channel_id=1, replica_groups=mesh['section'=2,'expert'=16,'tensor'=4] {'expert'}, dimensions={0} | all-to-all | bytes 3145728 | tf_op jit(solution)/shard_map/while/body/eval_jaxpr/all_to_all | solution.py:78
  300.2 61.7 %all-gather.2.cloned.1.call-done = bf16[16,64,3072]{2,1,0:T(8,128)(2,1)} async-done(((bf16[16,64,768]{2,1,0:T(8,128)(2,1)}), bf16[16,64,3072]{2,1,0:T(8,128)(2,1)}) %all-gather.2.cloned.1.call-update) | async-done | bytes 6291472 | tf_op jit(solution)/shard_map/while/body/eval_jaxpr/all_gather | solution.py:79
  361.9 8.0 %fusion.118 = (f32[16,64]{1,0:T(8,128)}, f32[16,64,512]{2,1,0:T(8,128)S(1)}) fusion(bf16[1,2,16,64,512]{4,3,2,1,0:T(8,128)(2,1)} %get-tuple-element.705, s32[]{:T(128)S(6)} %min.13, bf16[1,2,16,64,512]{4,3,2,1,0:T(8,128)(2,1)} %get-tuple-element.706, bf16[16,64,3072]{2,1,0:T(8,128)(2,1)} %all-gather.2.cloned.1.call-done, ...), kind=kOutput, calls=%fused_computation.17.clone.1 | convolution fusion | flops 3225943040 | bytes 13635588 | tf_op jit(solution)/shard_map/while/body/eval_jaxpr/scw,fw->scf/dot_general | solution.py:48
  369.9 7.1 fusion.124
  377.0 9.1 %add_convert_fusion.2 = bf16[16,64,3072]{2,1,0:T(8,128)(2,1)} fusion(f32[16,64,3072]{2,1,0:T(8,128)} %fusion.124, bf16[3072,512]{1,0:T(8,128)(2,1)S(1)} %copy-done.7, f32[16,64,512]{2,1,0:T(8,128)} %copy-done.10, bf16[1,2,16,64,512]{4,3,2,1,0:T(8,128)(2,1)S(1)} %copy-done.9, s32[]{:T(128)S(6)} %min.13), kind=kOutput, calls=%fused_computation.2.clone.1 | convolution fusion | flops 3231186944 | bytes 25165828 | tf_op jit(solution)/shard_map/while/body/eval_jaxpr/scf,df->scd/dot_general | solution.py:89
  386.2 6.8 all-to-all-start.1
  393.2 6.3 all-to-all-done.1
  400.1 3.7 all-to-all-start.3
  404.1 3.3 all-to-all-done.3
  408.0 3.5 all-to-all-start.2
  411.4 38.1 %reduce-scatter.2.cloned.1.call-done = bf16[16,64,768]{2,1,0:T(8,128)(2,1)} async-done(((bf16[16,64,3072]{2,1,0:T(8,128)(2,1)}), bf16[16,64,768]{2,1,0:T(8,128)(2,1)}) %reduce-scatter.2.cloned.1.call-update) | async-done | bytes 1572880 | tf_op jit(solution)/shard_map/while/body/eval_jaxpr/reduce_scatter | solution.py:91
  449.5 3.4 convert_element_type.262
  453.0 6.8 all-to-all-start.4
  460.8 5.7 psum.32
  466.9 40.5 %all-to-all-done.4 = f32[16,64,768]{2,1,0:T(8,128)S(1)} async-done(((f32[16,64,768]{2,1,0:T(8,128)}), f32[16,64,768]{2,1,0:T(8,128)S(1)}, u32[]{:S(2)}, u32[]{:S(2)}) %all-to-all-start.4) | async-done | bytes 3145760 | tf_op jit(solution)/shard_map/while/body/eval_jaxpr/all_to_all | solution.py:95
  509.2 6.5 psum.33
  515.7 1.8 fusion.127
  517.5 1.3 collective-permute-start
  518.8 5.8 collective-permute-done
  525.6 1.2 reduce-window.24
  528.3 1.2 convolution_convert_fusion.2
  529.6 25.6 %all_to_all.76 = bf16[16,64,768]{2,1,0:T(8,128)(2,1)} all-to-all(bf16[16,64,768]{2,1,0:T(8,128)(2,1)S(1)} %bitcast.176), channel_id=1, replica_groups=mesh['section'=2,'expert'=16,'tensor'=4] {'expert'}, dimensions={0} | all-to-all | bytes 3145728 | tf_op jit(solution)/shard_map/while/body/eval_jaxpr/all_to_all | solution.py:78
  555.3 61.7 %all-gather.2.cloned.1.call-done = bf16[16,64,3072]{2,1,0:T(8,128)(2,1)} async-done(((bf16[16,64,768]{2,1,0:T(8,128)(2,1)}), bf16[16,64,3072]{2,1,0:T(8,128)(2,1)}) %all-gather.2.cloned.1.call-update) | async-done | bytes 6291472 | tf_op jit(solution)/shard_map/while/body/eval_jaxpr/all_gather | solution.py:79
  617.0 8.0 %fusion.118 = (f32[16,64]{1,0:T(8,128)}, f32[16,64,512]{2,1,0:T(8,128)S(1)}) fusion(bf16[1,2,16,64,512]{4,3,2,1,0:T(8,128)(2,1)} %get-tuple-element.705, s32[]{:T(128)S(6)} %min.13, bf16[1,2,16,64,512]{4,3,2,1,0:T(8,128)(2,1)} %get-tuple-element.706, bf16[16,64,3072]{2,1,0:T(8,128)(2,1)} %all-gather.2.cloned.1.call-done, ...), kind=kOutput, calls=%fused_computation.17.clone.1 | convolution fusion | flops 3225943040 | bytes 13635588 | tf_op jit(solution)/shard_map/while/body/eval_jaxpr/scw,fw->scf/dot_general | solution.py:48
  625.0 7.1 fusion.124
  632.1 9.1 %add_convert_fusion.2 = bf16[16,64,3072]{2,1,0:T(8,128)(2,1)} fusion(f32[16,64,3072]{2,1,0:T(8,128)} %fusion.124, bf16[3072,512]{1,0:T(8,128)(2,1)S(1)} %copy-done.7, f32[16,64,512]{2,1,0:T(8,128)} %copy-done.10, bf16[1,2,16,64,512]{4,3,2,1,0:T(8,128)(2,1)S(1)} %copy-done.9, s32[]{:T(128)S(6)} %min.13), kind=kOutput, calls=%fused_computation.2.clone.1 | convolution fusion | flops 3231186944 | bytes 25165828 | tf_op jit(solution)/shard_map/while/body/eval_jaxpr/scf,df->scd/dot_general | solution.py:89
  641.2 6.8 all-to-all-start.1
  648.2 6.3 all-to-all-done.1
  655.1 3.7 all-to-all-start.3
  659.1 3.3 all-to-all-done.3
  663.0 3.5 all-to-all-start.2
  666.5 38.1 %reduce-scatter.2.cloned.1.call-done = bf16[16,64,768]{2,1,0:T(8,128)(2,1)} async-done(((bf16[16,64,3072]{2,1,0:T(8,128)(2,1)}), bf16[16,64,768]{2,1,0:T(8,128)(2,1)}) %reduce-scatter.2.cloned.1.call-update) | async-done | bytes 1572880 | tf_op jit(solution)/shard_map/while/body/eval_jaxpr/reduce_scatter | solution.py:91
  704.6 3.4 convert_element_type.262
  708.0 6.8 all-to-all-start.4
  715.9 5.7 psum.32
  722.0 40.5 %all-to-all-done.4 = f32[16,64,768]{2,1,0:T(8,128)S(1)} async-done(((f32[16,64,768]{2,1,0:T(8,128)}), f32[16,64,768]{2,1,0:T(8,128)S(1)}, u32[]{:S(2)}, u32[]{:S(2)}) %all-to-all-start.4) | async-done | bytes 3145760 | tf_op jit(solution)/shard_map/while/body/eval_jaxpr/all_to_all | solution.py:95
  764.3 6.5 psum.33
  770.8 1.8 fusion.127
  772.6 1.3 collective-permute-start
  773.9 5.8 collective-permute-done
  (201 shorter events, 23.6 us)
Async XLA Ops:
  8.0 98.9 %all-gather.2.cloned.1.call-start = ((), (), s32[]{:S(2)}) async-start(), calls=%async_computation.6 | async-start | bytes 7864320 | tf_op jit(solution)/shard_map/while/body/eval_jaxpr/all_gather | solution.py:79
  13.0 93.8 %copy-start.5 = (bf16[512,3072]{1,0:T(8,128)(2,1)S(1)}, bf16[512,3072]{1,0:T(8,128)(2,1)}, u32[]{:S(2)}) copy-start(bf16[512,3072]{1,0:T(8,128)(2,1)} %get-tuple-element.704) | copy-start | bytes 9437188 | tf_op jit(solution)/shard_map/while
  43.5 151.0 %reduce-scatter.2.cloned.1.call-start = ((), (), s32[]{:S(2)}) async-start(), calls=%async_computation.7 | async-start | bytes 7864320 | tf_op jit(solution)/shard_map/while/body/eval_jaxpr/reduce_scatter | solution.py:91
  106.8 8.0 %copy-start.6 = (bf16[3072,512]{1,0:T(8,128)(2,1)S(1)}, bf16[3072,512]{1,0:T(8,128)(2,1)}, u32[]{:S(2)}) copy-start(bf16[3072,512]{1,0:T(8,128)(2,1)} %get-tuple-element.707) | copy-start | bytes 9437188 | tf_op jit(solution)/shard_map/while
  106.8 8.0 %copy-start.8 = (bf16[1,2,16,64,512]{4,3,2,1,0:T(8,128)(2,1)S(1)}, bf16[1,2,16,64,512]{4,3,2,1,0:T(8,128)(2,1)}, u32[]{:S(2)}) copy-start(bf16[1,2,16,64,512]{4,3,2,1,0:T(8,128)(2,1)} %get-tuple-element.705) | copy-start | bytes 6291460 | tf_op jit(solution)/shard_map/while
  106.8 8.0 %copy-start.9 = (bf16[1,2,16,64,512]{4,3,2,1,0:T(8,128)(2,1)S(1)}, bf16[1,2,16,64,512]{4,3,2,1,0:T(8,128)(2,1)}, u32[]{:S(2)}) copy-start(bf16[1,2,16,64,512]{4,3,2,1,0:T(8,128)(2,1)} %get-tuple-element.706) | copy-start | bytes 6291460 | tf_op jit(solution)/shard_map/while
  114.8 7.2 copy-start.10
  114.8 7.2 copy-start.7
  131.1 6.9 copy-start
  131.1 13.3 %all-to-all-start.1 = ((f32[16,1,64]{2,1,0:T(1,128)}), f32[16,1,64]{2,1,0:T(1,128)S(1)}, u32[]{:S(2)}, u32[]{:S(2)}) async-start(f32[16,1,64]{2,1,0:T(1,128)} %bitcast.169), calls=%async_computation.1 | async-start | bytes 16384 | tf_op jit(solution)/shard_map/while/body/eval_jaxpr/all_to_all | solution.py:96
  145.0 7.3 all-to-all-start.3
  152.9 45.0 %all-to-all-start.2 = ((f32[4,80,2]{1,2,0:T(2,128)}), f32[4,80,2]{1,2,0:T(2,128)S(1)}, u32[]{:S(2)}, u32[]{:S(2)}) async-start(f32[4,80,2]{1,2,0:T(2,128)} %broadcast_in_dim.101), calls=%async_computation.2 | async-start | bytes 8192 | tf_op jit(solution)/shard_map/while/body/eval_jaxpr/all_to_all | solution.py:12
  197.9 6.9 copy-start.4
  197.9 7.7 copy-start.3
  197.9 54.5 %all-to-all-start.4 = ((f32[16,64,768]{2,1,0:T(8,128)}), f32[16,64,768]{2,1,0:T(8,128)S(1)}, u32[]{:S(2)}, u32[]{:S(2)}) async-start(f32[16,64,768]{2,1,0:T(8,128)} %convert_element_type.262), calls=%async_computation.5 | async-start | bytes 6291456 | tf_op jit(solution)/shard_map/while/body/eval_jaxpr/all_to_all | solution.py:95
  252.4 0.9 copy-start.1
  252.4 1.0 copy-start.2
  262.5 7.1 collective-permute-start
  269.6 92.3 %all-gather.2.cloned.1.call-start = ((), (), s32[]{:S(2)}) async-start(), calls=%async_computation.6 | async-start | bytes 7864320 | tf_op jit(solution)/shard_map/while/body/eval_jaxpr/all_gather | solution.py:79
  274.6 87.3 %copy-start.5 = (bf16[512,3072]{1,0:T(8,128)(2,1)S(1)}, bf16[512,3072]{1,0:T(8,128)(2,1)}, u32[]{:S(2)}) copy-start(bf16[512,3072]{1,0:T(8,128)(2,1)} %get-tuple-element.704) | copy-start | bytes 9437188 | tf_op jit(solution)/shard_map/while
  300.2 149.3 %reduce-scatter.2.cloned.1.call-start = ((), (), s32[]{:S(2)}) async-start(), calls=%async_computation.7 | async-start | bytes 7864320 | tf_op jit(solution)/shard_map/while/body/eval_jaxpr/reduce_scatter | solution.py:91
  361.9 8.0 %copy-start.6 = (bf16[3072,512]{1,0:T(8,128)(2,1)S(1)}, bf16[3072,512]{1,0:T(8,128)(2,1)}, u32[]{:S(2)}) copy-start(bf16[3072,512]{1,0:T(8,128)(2,1)} %get-tuple-element.707) | copy-start | bytes 9437188 | tf_op jit(solution)/shard_map/while
  361.9 8.0 %copy-start.8 = (bf16[1,2,16,64,512]{4,3,2,1,0:T(8,128)(2,1)S(1)}, bf16[1,2,16,64,512]{4,3,2,1,0:T(8,128)(2,1)}, u32[]{:S(2)}) copy-start(bf16[1,2,16,64,512]{4,3,2,1,0:T(8,128)(2,1)} %get-tuple-element.705) | copy-start | bytes 6291460 | tf_op jit(solution)/shard_map/while
  361.9 8.0 %copy-start.9 = (bf16[1,2,16,64,512]{4,3,2,1,0:T(8,128)(2,1)S(1)}, bf16[1,2,16,64,512]{4,3,2,1,0:T(8,128)(2,1)}, u32[]{:S(2)}) copy-start(bf16[1,2,16,64,512]{4,3,2,1,0:T(8,128)(2,1)} %get-tuple-element.706) | copy-start | bytes 6291460 | tf_op jit(solution)/shard_map/while
  369.9 7.2 copy-start.10
  369.9 7.2 copy-start.7
  386.2 6.9 copy-start
  386.2 13.3 %all-to-all-start.1 = ((f32[16,1,64]{2,1,0:T(1,128)}), f32[16,1,64]{2,1,0:T(1,128)S(1)}, u32[]{:S(2)}, u32[]{:S(2)}) async-start(f32[16,1,64]{2,1,0:T(1,128)} %bitcast.169), calls=%async_computation.1 | async-start | bytes 16384 | tf_op jit(solution)/shard_map/while/body/eval_jaxpr/all_to_all | solution.py:96
  400.1 7.3 all-to-all-start.3
  408.0 45.0 %all-to-all-start.2 = ((f32[4,80,2]{1,2,0:T(2,128)}), f32[4,80,2]{1,2,0:T(2,128)S(1)}, u32[]{:S(2)}, u32[]{:S(2)}) async-start(f32[4,80,2]{1,2,0:T(2,128)} %broadcast_in_dim.101), calls=%async_computation.2 | async-start | bytes 8192 | tf_op jit(solution)/shard_map/while/body/eval_jaxpr/all_to_all | solution.py:12
  453.0 6.9 copy-start.4
  453.0 7.7 copy-start.3
  453.0 54.5 %all-to-all-start.4 = ((f32[16,64,768]{2,1,0:T(8,128)}), f32[16,64,768]{2,1,0:T(8,128)S(1)}, u32[]{:S(2)}, u32[]{:S(2)}) async-start(f32[16,64,768]{2,1,0:T(8,128)} %convert_element_type.262), calls=%async_computation.5 | async-start | bytes 6291456 | tf_op jit(solution)/shard_map/while/body/eval_jaxpr/all_to_all | solution.py:95
  507.5 0.9 copy-start.1
  507.5 1.0 copy-start.2
  517.5 7.1 collective-permute-start
  524.6 92.3 %all-gather.2.cloned.1.call-start = ((), (), s32[]{:S(2)}) async-start(), calls=%async_computation.6 | async-start | bytes 7864320 | tf_op jit(solution)/shard_map/while/body/eval_jaxpr/all_gather | solution.py:79
  529.6 87.3 %copy-start.5 = (bf16[512,3072]{1,0:T(8,128)(2,1)S(1)}, bf16[512,3072]{1,0:T(8,128)(2,1)}, u32[]{:S(2)}) copy-start(bf16[512,3072]{1,0:T(8,128)(2,1)} %get-tuple-element.704) | copy-start | bytes 9437188 | tf_op jit(solution)/shard_map/while
  555.3 149.3 %reduce-scatter.2.cloned.1.call-start = ((), (), s32[]{:S(2)}) async-start(), calls=%async_computation.7 | async-start | bytes 7864320 | tf_op jit(solution)/shard_map/while/body/eval_jaxpr/reduce_scatter | solution.py:91
  617.0 8.0 %copy-start.6 = (bf16[3072,512]{1,0:T(8,128)(2,1)S(1)}, bf16[3072,512]{1,0:T(8,128)(2,1)}, u32[]{:S(2)}) copy-start(bf16[3072,512]{1,0:T(8,128)(2,1)} %get-tuple-element.707) | copy-start | bytes 9437188 | tf_op jit(solution)/shard_map/while
  617.0 8.0 %copy-start.8 = (bf16[1,2,16,64,512]{4,3,2,1,0:T(8,128)(2,1)S(1)}, bf16[1,2,16,64,512]{4,3,2,1,0:T(8,128)(2,1)}, u32[]{:S(2)}) copy-start(bf16[1,2,16,64,512]{4,3,2,1,0:T(8,128)(2,1)} %get-tuple-element.705) | copy-start | bytes 6291460 | tf_op jit(solution)/shard_map/while
  617.0 8.0 %copy-start.9 = (bf16[1,2,16,64,512]{4,3,2,1,0:T(8,128)(2,1)S(1)}, bf16[1,2,16,64,512]{4,3,2,1,0:T(8,128)(2,1)}, u32[]{:S(2)}) copy-start(bf16[1,2,16,64,512]{4,3,2,1,0:T(8,128)(2,1)} %get-tuple-element.706) | copy-start | bytes 6291460 | tf_op jit(solution)/shard_map/while
  624.9 7.2 copy-start.10
  625.0 7.2 copy-start.7
  641.2 6.9 copy-start
  641.2 13.3 %all-to-all-start.1 = ((f32[16,1,64]{2,1,0:T(1,128)}), f32[16,1,64]{2,1,0:T(1,128)S(1)}, u32[]{:S(2)}, u32[]{:S(2)}) async-start(f32[16,1,64]{2,1,0:T(1,128)} %bitcast.169), calls=%async_computation.1 | async-start | bytes 16384 | tf_op jit(solution)/shard_map/while/body/eval_jaxpr/all_to_all | solution.py:96
  655.1 7.3 all-to-all-start.3
  663.0 45.0 %all-to-all-start.2 = ((f32[4,80,2]{1,2,0:T(2,128)}), f32[4,80,2]{1,2,0:T(2,128)S(1)}, u32[]{:S(2)}, u32[]{:S(2)}) async-start(f32[4,80,2]{1,2,0:T(2,128)} %broadcast_in_dim.101), calls=%async_computation.2 | async-start | bytes 8192 | tf_op jit(solution)/shard_map/while/body/eval_jaxpr/all_to_all | solution.py:12
  708.0 6.9 copy-start.4
  708.0 7.7 copy-start.3
  708.0 54.5 %all-to-all-start.4 = ((f32[16,64,768]{2,1,0:T(8,128)}), f32[16,64,768]{2,1,0:T(8,128)S(1)}, u32[]{:S(2)}, u32[]{:S(2)}) async-start(f32[16,64,768]{2,1,0:T(8,128)} %convert_element_type.262), calls=%async_computation.5 | async-start | bytes 6291456 | tf_op jit(solution)/shard_map/while/body/eval_jaxpr/all_to_all | solution.py:95
  762.5 0.9 copy-start.1
  762.5 1.0 copy-start.2
  772.6 7.1 collective-permute-start
Sparse Core Ops, SparseCore 0:
  43.6 63.1 all-gather.1
  131.2 63.1 reduce-scatter.1
  300.3 61.5 all-gather.1
  386.3 63.1 reduce-scatter.1
  555.4 61.5 all-gather.1
  641.4 63.1 reduce-scatter.1
where the time goes:
time: 789 us; the launch traced here: 787 us
  waiting for transfers between devices  469 us (59%)
  blocking collectives  118 us (15%)
  matrix products  80.6 us (10%)
  starting transfers between devices  66.6 us (8%)
  other arithmetic  26.5 us (3%)
  between operations  13.4 us (2%)
  local copies, waits for them, and re-layouts  11.9 us (2%)
    all_gather x3, waiting for transfers between devices, layer_back(): lax.all_gather(arrived, 'tensor', axis=2, tiled=True)  187 us
    all_to_all x3, waiting for transfers between devices, layer_back(): lax.all_to_all(unit_share, 'expert', split_axis=0, concat_axis=0, tiled=T...  122 us
    reduce_scatter x3, waiting for transfers between devices, layer_back(): lax.psum_scatter(unit.astype(jnp.bfloat16), 'tensor', scatter_dimension=2...  114 us
    all_to_all x3, blocking collectives, layer_back(): lax.all_to_all(copies, 'expert', split_axis=0, concat_axis=0, tiled=True)  81.6 us
    dot_general x3, matrix products, layer_back(): jnp.einsum('scf,df->scd', up_grad, up_mat, preferred_element_type=jnp.flo...  27.3 us
    dot_general x3, matrix products, add_columns(): jnp.einsum('scw,fw->scf', piece, down_mat, preferred_element_type=jnp.flo...  23.9 us
    all_to_all x6, starting transfers between devices, from_everyone(): return lax.all_to_all(copies, axis, split_axis=0, concat_axis=0, tiled=True)  21.5 us
    dot_general x3, matrix products, layer_back(): jnp.einsum('scf,df->scd', gate_grad, gate_mat, preferred_element_type=jnp...  21.4 us
  transfers between devices with their start and end apart: 21, of which 18 were waited for; matrix products, arithmetic and copies ran while one was open for 2% of the time, Pallas kernels for 0%

commit v1 on v0

v1 whole, which is shorter than its diff:
```python
import functools
import jax
import jax.numpy as jnp
from jax import lax
from jax.experimental import pallas as pl
from jax.experimental.pallas import tpu as pltpu
from jax.sharding import PartitionSpec as P

norm_eps = 1e-05
OFF = (0, -1, 1, 2)
MESH = pl.DeviceIdType.MESH
NT = (((1,), (1,)), ((), ()))


def kernel(
    sections, n, sizes,
    gout, xin, scale, gain, info_h, sg_h, su_h, wd_h, wg_h, wu_h, rp_h,
    out,
    G, U, D, RH, RF, RHF, RFF, RX, hop, mrecv, msend,
    V, A, B, bt, DC, wd, wc, info, sg, su,
    ld, x_s, x_r, fo_s, fo_r, ff_s, ff_r, so_s, so_r, sf_s, sf_r, dd_s, dd_r,
    e_s, e_r, rh_s, rh_r, rf_s, rf_r, hf_s, hf_r, ff2_s, ff2_r, rx_s, rx_r,
    m_s, m_r, hop_s, hop_r, gate,
):
    micros, T, Q, F, cap, lanes = sizes
    width = 4 * Q
    K = 2 * F + lanes
    sec = lax.axis_index("section")
    ex = lax.axis_index("expert")
    te = lax.axis_index("tensor")
    z, y = ex // n, ex % n
    xl, c = te // 2, te % 2
    fp = y * (1 - c) + z * c
    sp = z * (1 - c) + y * c

    def at(v, o):
        return lax.rem(v + o + n, n)

    def exid(f, s):
        return (1 - c) * (s * n + f) + c * (f * n + s)

    partner = {"tensor": xl * 2 + 1 - c}
    xnbr = {"tensor": (1 - xl) * 2 + c}
    xdiag = {"tensor": (1 - xl) * 2 + 1 - c}
    fdir = ({"expert": exid(at(fp, 1), sp)}, {"expert": exid(at(fp, -1), sp)})
    sdir = ({"expert": exid(fp, at(sp, 1))}, {"expert": exid(fp, at(sp, -1))})
    hoppeer = {"section": 1 - sec, "tensor": (1 - xl) * 2 + c}
    near = (partner, xnbr, xdiag) + fdir + sdir

    def load(k, src, dst):
        return pltpu.make_async_copy(src, dst, ld.at[k])

    def weight_loads():
        return (
            load(0, wd_h, wd),
            load(1, wg_h, wc.at[:, pl.ds(0, F)]),
            load(2, wu_h, wc.at[:, pl.ds(F, F)]),
            load(3, rp_h, wc.at[:, pl.ds(2 * F, lanes)]),
        )

    for cp in weight_loads():
        cp.start()

    barrier = pltpu.get_barrier_semaphore()
    greeted = near + ((hoppeer,) if sections == 2 else ())
    for peer in greeted:
        pl.semaphore_signal(barrier, inc=1, device_id=peer, device_id_type=MESH)
    pl.semaphore_wait(barrier, len(greeted))

    def rc(src, dst, ss, rs, peer):
        return pltpu.make_async_remote_copy(
            src_ref=src, dst_ref=dst, send_sem=ss, recv_sem=rs, device_id=peer, device_id_type=MESH
        )

    def one_micro(m, carry):
        @pl.when(m > 0)
        def _():
            for peer in near:
                pl.semaphore_signal(gate, inc=1, device_id=peer, device_id_type=MESH)
            pl.semaphore_wait(gate, len(near))

        small = (
            load(4, info_h.at[m], info),
            load(5, sg_h.at[m], sg),
            load(6, su_h.at[m], su),
        )
        for cp in small:
            cp.start()
        sent = []

        def go(*a):
            cp = rc(*a)
            cp.start()
            sent.append(cp)

        def got(ref, ss, rs, peer):
            rc(ref, ref, ss, rs, peer).wait_recv()

        top = sec == sections - 1
        qh = jnp.where(top, xl, 1 - xl)
        qo = 1 - qh
        mine = G.at[c, sp, fp]

        @pl.when(top)
        def _():
            G[c, sp, fp, qh] = gout[m]

        if sections == 2:

            @pl.when(jnp.logical_not(top))
            def _():
                got(hop.at[m], hop_s.at[m], hop_r.at[m], hoppeer)
                G[c, sp, fp, qh] = hop[m]

        go(mine.at[qh], mine.at[qh], x_s, x_r, xnbr)
        for d in range(2):
            go(mine.at[qh], mine.at[qh], fo_s.at[0, d], fo_r.at[0, d], fdir[d])
        V[...] = jnp.zeros_like(V)
        got(mine.at[qo], x_s, x_r, xnbr)
        for d in range(2):
            go(mine.at[qo], mine.at[qo], fo_s.at[1, d], fo_r.at[1, d], fdir[d])

        def spread(k, slot):
            for d in range(2):
                go(slot, slot, so_s.at[k, d], so_r.at[k, d], sdir[d])

        def share(kk, k, slot):
            go(slot, slot, dd_s.at[kk, k], dd_r.at[kk, k], partner)

        spread(0, mine)
        share(0, 0, mine)
        for cp in small:
            cp.wait()

        @pl.when(m == 0)
        def _():
            for cp in weight_loads():
                cp.wait()

        def prepare(j, carry):
            i0, i1 = j // n, j % n
            pos = info[i0, i1, :, 0:1]
            slots = lax.broadcasted_iota(jnp.int32, (T, cap), 1).astype(jnp.float32)
            place = jnp.where(slots == pos, 1.0, 0.0).astype(jnp.bfloat16)
            a = jnp.dot(place, sg[j], preferred_element_type=jnp.float32)
            b = jnp.dot(place, su[j], preferred_element_type=jnp.float32)
            sig = jax.nn.sigmoid(a)
            A[i0, i1] = b * sig * (1.0 + a * (1.0 - sig))
            B[i0, i1] = a * sig
            bt[i0, i1] = b.astype(jnp.bfloat16)
            return carry

        def prepare_rows(i):
            lax.fori_loop(i * n, (i + 1) * n, prepare, 0)

        def into_v(kk):
            for k in range(n):
                ref = G.at[1 - c, at(fp, OFF[kk]), at(sp, OFF[k])]
                got(ref, dd_s.at[kk, k], dd_r.at[kk, k], partner)
            zi, yi = at(z, OFF[kk]), at(y, OFF[kk])
            for h in range(2):
                part = jnp.zeros((n * T, F), jnp.float32)
                for q in range(2):
                    g = (G[0, zi, :, q] if h == 0 else G[1, yi, :, q]).reshape(n * T, Q)
                    w = wd[:, (2 * q + h) * Q : (2 * q + h + 1) * Q]
                    part = part + lax.dot_general(g, w, NT, preferred_element_type=jnp.float32)
                part = part.reshape(n, T, F)
                if h == 0:
                    V[zi] += part
                else:
                    V[:, yi] += part

        prepare_rows(0)
        for d in range(2):
            f = at(fp, -1 if d == 0 else 1)
            slot = G.at[c, sp, f]
            for i, q in enumerate((qh, qo)):
                got(slot.at[q], fo_s.at[i, d], fo_r.at[i, d], fdir[d])
            go(slot.at[d], slot.at[d], ff_s.at[d], ff_r.at[d], fdir[d])
            spread(1 + d, slot)
            share(0, 1 + d, slot)
        far = G.at[c, sp, at(fp, 2)]
        for d in range(2):
            got(far.at[d], ff_s.at[d], ff_r.at[d], fdir[d])
        spread(3, far)
        share(0, 3, far)

        def pass_on(k):
            f = at(fp, OFF[k])
            for d in range(2):
                slot = G.at[c, at(sp, -1 if d == 0 else 1), f]
                got(slot, so_s.at[k, d], so_r.at[k, d], sdir[d])
                go(slot.at[d], slot.at[d], sf_s.at[k, d], sf_r.at[k, d], sdir[d])
                share(1 + d, k, slot)

        pass_on(0)
        prepare_rows(1)
        pass_on(1)
        into_v(0)
        pass_on(2)
        prepare_rows(2)
        pass_on(3)
        prepare_rows(3)
        for k in range(n):
            slot = G.at[c, at(sp, 2), at(fp, OFF[k])]
            for d in range(2):
                got(slot.at[d], sf_s.at[k, d], sf_r.at[k, d], sdir[d])
            share(3, k, slot)
            if k == 1:
                into_v(1)
            if k == 2:
                into_v(2)
        into_v(3)

        def finish(j, carry):
            i0, i1 = j // n, j % n
            v = V[i0, i1]
            db = v * B[i0, i1]
            w = jnp.sum(db * bt[i0, i1].astype(jnp.float32), axis=-1, keepdims=True)
            row = info[i0, i1]
            DC[i0, i1, :, 0:F] = (v * A[i0, i1]).astype(jnp.bfloat16)
            DC[i0, i1, :, F : 2 * F] = db.astype(jnp.bfloat16)
            DC[i0, i1, :, 2 * F :] = (w * row[:, 2:3] * row).astype(jnp.bfloat16)
            return carry

        lax.fori_loop(0, n * n, finish, 0)

        def into_u(kk):
            zi, yi = at(z, OFF[kk]), at(y, OFF[kk])
            for h in range(2):
                da = (DC[zi] if h == 0 else DC[:, yi]).reshape(n * T, K)
                q_own = (info[zi, :, :, 1:2] if h == 0 else info[:, yi, :, 1:2]).reshape(n * T, 1)

                def half(q, carry):
                    low = pl.multiple_of((2 * q + h) * Q, Q)
                    u = lax.dot_general(
                        da, wc[pl.ds(low, Q), :], NT, preferred_element_type=jnp.float32
                    )
                    u = (u * q_own).astype(jnp.bfloat16).reshape(n, T, Q)
                    U[h, zi if h == 0 else yi, :, q] = u
                    return carry

                lax.fori_loop(0, 2, half, 0)
            go(U.at[1 - c, at(fp, OFF[kk])], D.at[kk], e_s.at[kk], e_r.at[kk], partner)

        def add_partner(kk):
            got(D.at[kk], e_s.at[kk], e_r.at[kk], partner)
            i = at(sp, OFF[kk])
            U[c, i] = U[c, i] + D[kk]

        into_u(3)
        add_partner(3)
        s2 = at(sp, 2)
        for d in range(2):
            go(U.at[c, s2, :, d], RH.at[d], rh_s.at[d], rh_r.at[d], sdir[d])
        into_u(2)
        add_partner(2)
        into_u(1)
        add_partner(1)
        for d in range(2):
            i = at(sp, 1 if d == 0 else -1)
            got(RH.at[d], rh_s.at[d], rh_r.at[d], sdir[d])
            U[c, i, :, d] = U[c, i, :, d] + RH[d]
            for k in (3, 2, 1, 0):
                f = at(fp, OFF[k])
                go(U.at[c, i, f], RF.at[d, k], rf_s.at[d, k], rf_r.at[d, k], sdir[d])
        into_u(0)
        add_partner(0)

        def own_sum(k):
            for d in range(2):
                got(RF.at[d, k], rf_s.at[d, k], rf_r.at[d, k], sdir[d])
            f = at(fp, OFF[k])
            total = U[c, sp, f].astype(jnp.float32) + RF[0, k].astype(jnp.float32)
            U[c, sp, f] = (total + RF[1, k].astype(jnp.float32)).astype(jnp.bfloat16)

        own_sum(3)
        f2 = at(fp, 2)
        for d in range(2):
            go(U.at[c, sp, f2, d], RHF.at[d], hf_s.at[d], hf_r.at[d], fdir[d])
        for d, k in ((0, 2), (1, 1)):
            own_sum(k)
            f = at(fp, OFF[k])
            got(RHF.at[d], hf_s.at[d], hf_r.at[d], fdir[d])
            U[c, sp, f, d] = U[c, sp, f, d] + RHF[d]
            go(U.at[c, sp, f], RFF.at[d], ff2_s.at[d], ff2_r.at[d], fdir[d])
        own_sum(0)
        for d in range(2):
            got(RFF.at[d], ff2_s.at[d], ff2_r.at[d], fdir[d])

        def three(q):
            total = U[c, sp, fp, q].astype(jnp.float32) + RFF[0, q].astype(jnp.float32)
            return total + RFF[1, q].astype(jnp.float32)

        U[c, sp, fp, 1 - xl] = three(1 - xl).astype(jnp.bfloat16)
        go(U.at[c, sp, fp, 1 - xl], RX, rx_s, rx_r, xnbr)
        dn = three(xl)
        got(RX, rx_s, rx_r, xnbr)
        dn = dn + RX[...].astype(jnp.float32)

        gained = dn * gain[...]
        values = xin[m].astype(jnp.float32)
        part = jnp.sum(values * gained, axis=-1, keepdims=True)
        msend[...] = jnp.broadcast_to(part, msend.shape)
        for i, peer in enumerate((partner, xnbr, xdiag)):
            go(msend, mrecv.at[i], m_s.at[i], m_r.at[i], peer)
        for i, peer in enumerate((partner, xnbr, xdiag)):
            got(mrecv.at[i], m_s.at[i], m_r.at[i], peer)
        moment = (msend[...] + mrecv[0] + mrecv[1] + mrecv[2])[:, 0:1] / width
        sc = scale[m][:, 0:1]
        result = G[c, sp, fp, xl].astype(jnp.float32) + sc * gained - values * (sc * sc * sc * moment)
        out[m] = result.astype(jnp.bfloat16)
        if sections == 2:

            @pl.when(top)
            def _():
                rc(out.at[m], hop.at[m], hop_s.at[m], hop_r.at[m], hoppeer).start()

        for cp in sent:
            cp.wait_send()
        if sections == 2:

            @pl.when(top)
            def _():
                rc(out.at[m], hop.at[m], hop_s.at[m], hop_r.at[m], hoppeer).wait_send()

        return carry

    lax.fori_loop(0, micros, one_micro, 0)


def on_device(
    layer_inputs, grad_out, norm_gain, router_w, w_gate, w_up, w_down, saved_gate, saved_up, routes
):
    sections = lax.axis_size("section")
    holders = lax.axis_size("expert")
    n = 4
    micros, T, Q = grad_out.shape
    F = w_gate.shape[2]
    cap = saved_gate.shape[3]
    lanes = 128
    router = router_w[0]
    experts = router.shape[1]
    width = w_gate.shape[1]
    own = lax.axis_index("expert") // (holders // experts)
    gain_full = norm_gain.astype(jnp.float32)
    expert_ids = jnp.arange(experts, dtype=jnp.int32)

    values = layer_inputs[0].astype(jnp.float32)
    squares = lax.psum(jnp.sum(values * values, axis=-1), "tensor")
    scale = lax.rsqrt(squares / width + norm_eps)[:, :, None]
    normed = (values * scale * gain_full).astype(jnp.bfloat16)
    logits = lax.psum(jnp.dot(normed, router, preferred_element_type=jnp.float32), "tensor")
    chosen = routes[0]
    onehot = (chosen[..., None] == expert_ids).astype(jnp.float32)
    picked = jnp.sum(onehot * logits[:, :, None, :], axis=-1)
    delta = picked[..., 0] - picked[..., 1]
    packed = jnp.concatenate([chosen.astype(jnp.float32), delta[..., None]], axis=-1)
    packed = jnp.swapaxes(lax.all_gather(packed, "expert"), 0, 1)
    named = packed[..., :2].astype(jnp.int32)
    q0, q1 = jax.nn.sigmoid(packed[..., 2]), jax.nn.sigmoid(-packed[..., 2])
    is0, is1 = named[..., 0] == own, named[..., 1] == own
    used = jnp.logical_or(is0, is1)
    count = used.astype(jnp.float32)
    earlier = jnp.tril(jnp.ones((T, T), jnp.float32), -1)
    pos = jnp.einsum("mbt,ut->mbu", count, earlier)
    pos = jnp.where(used, pos, -1.0)
    q_own = jnp.where(is0, q0, jnp.where(is1, q1, 0.0))
    q_other = jnp.where(is0, q1, jnp.where(is1, -q0, 0.0))
    sign = (named[..., 0:1] == expert_ids).astype(jnp.float32) - (
        named[..., 1:2] == expert_ids
    ).astype(jnp.float32)
    info = jnp.concatenate([pos[..., None], q_own[..., None], q_other[..., None], sign], axis=-1)
    info = jnp.pad(info, ((0, 0), (0, 0), (0, 0), (0, lanes - info.shape[-1])))
    info = info.reshape(micros, n, n, T, lanes)
    router_all = lax.all_gather(router, "tensor", axis=0, tiled=True)
    rp = jnp.pad(router_all, ((0, 0), (3, lanes - 3 - experts)))
    scale_wide = jnp.broadcast_to(scale, (micros, T, lanes))

    bf, f32 = jnp.bfloat16, jnp.float32
    vm = pl.BlockSpec(memory_space=pltpu.VMEM)
    anym = pl.BlockSpec(memory_space=pl.ANY)
    dma = pltpu.SemaphoreType.DMA
    K = 2 * F + lanes
    grads = pl.pallas_call(
        functools.partial(kernel, sections, n, (micros, T, Q, F, cap, lanes)),
        out_shape=jax.ShapeDtypeStruct((micros, T, Q), bf),
        in_specs=[vm] * 4 + [anym] * 7,
        out_specs=vm,
        scratch_shapes=[
            pltpu.VMEM((2, n, n, 2, T, Q), bf),
            pltpu.VMEM((2, n, n, 2, T, Q), bf),
            pltpu.VMEM((n, n, 2, T, Q), bf),
            pltpu.VMEM((2, n, T, Q), bf),
            pltpu.VMEM((2, n, 2, T, Q), bf),
            pltpu.VMEM((2, T, Q), bf),
            pltpu.VMEM((2, 2, T, Q), bf),
            pltpu.VMEM((T, Q), bf),
            pltpu.VMEM((micros, T, Q), bf),
            pltpu.VMEM((3, T, lanes), f32),
            pltpu.VMEM((T, lanes), f32),
            pltpu.VMEM((n, n, T, F), f32),
            pltpu.VMEM((n, n, T, F), f32),
            pltpu.VMEM((n, n, T, F), f32),
            pltpu.VMEM((n, n, T, F), bf),
            pltpu.VMEM((n, n, T, K), bf),
            pltpu.VMEM((F, width), bf),
            pltpu.VMEM((width, K), bf),
            pltpu.VMEM((n, n, T, lanes), f32),
            pltpu.VMEM((n * n, cap, F), bf),
            pltpu.VMEM((n * n, cap, F), bf),
            dma((7,)),
            dma, dma,
            dma((2, 2)), dma((2, 2)), dma((2,)), dma((2,)),
            dma((4, 2)), dma((4, 2)), dma((4, 2)), dma((4, 2)),
            dma((4, 4)), dma((4, 4)),
            dma((4,)), dma((4,)), dma((2,)), dma((2,)), dma((2, 4)), dma((2, 4)),
            dma((2,)), dma((2,)), dma((2,)), dma((2,)), dma, dma,
            dma((3,)), dma((3,)), dma((micros,)), dma((micros,)),
            pltpu.SemaphoreType.REGULAR,
        ],
        compiler_params=pltpu.CompilerParams(
            collective_id=0, has_side_effects=True, vmem_limit_bytes=66_000_000
        ),
        name="layer_back",
    )(
        grad_out, layer_inputs[0], scale_wide, gain_full, info, saved_gate[0], saved_up[0],
        w_down[0], w_gate[0], w_up[0], rp,
    )
    return grads[None]


def solution(mesh):
    placed = (
        P("section", None, "expert", "tensor"),
        P(None, "expert", "tensor"),
        P("section", "tensor"),
        P("section", "tensor", None),
        P("section", None, ("expert", "tensor")),
        P("section", None, ("expert", "tensor")),
        P("section", ("expert", "tensor"), None),
        P("section", None, None, None, ("expert", "tensor")),
        P("section", None, None, None, ("expert", "tensor")),
        P("section", None, "expert", None),
    )
    return jax.shard_map(
        on_device,
        mesh=mesh,
        in_specs=placed,
        out_specs=P("section", None, "expert", "tensor"),
        check_vma=False,
    )
```

time: 789 us -> 300 us (0.38)
  waiting for transfers between devices: 469 us -> 0 us
  Pallas kernels: 0 us -> 242 us
  matrix products: 80.6 us -> 1.36 us
  blocking collectives: 118 us -> 46.8 us
  starting transfers between devices: 66.6 us -> 0 us
  other arithmetic: 26.5 us -> 3.89 us
  between operations: 13.4 us -> 0.1 us
    pallas_call x0 -> x1, Pallas kernels: none -> 242 us  [on_device(): pl.pallas_call(functools.partial(kernel, sections, n, (micros, T, Q, F, c...]
    all_gather x3 -> x0, waiting for transfers between devices: 187 us -> none  [layer_back(): lax.all_gather(arrived, 'tensor', axis=2, tiled=True)]
    all_to_all x12 -> x0, waiting for transfers between devices: 150 us -> none  [the longest x3 122 us: layer_back(): lax.all_to_all(unit_share, 'expert', split_axis=0, concat_axis=0, tiled=T...]
    reduce_scatter x3 -> x0, waiting for transfers between devices: 114 us -> none  [layer_back(): lax.psum_scatter(unit.astype(jnp.bfloat16), 'tensor', scatter_dimension=2...]
    all_to_all x3 -> x0, blocking collectives: 81.6 us -> none  [layer_back(): lax.all_to_all(copies, 'expert', split_axis=0, concat_axis=0, tiled=True)]
    dot_general x24 -> x2, matrix products: 80.6 us -> 1.36 us  [the longest x1 1.16 us: on_device(): jnp.dot(normed, router, preferred_element_type=jnp.float32)]
    all_to_all x12 -> x0, starting transfers between devices: 62.6 us -> none  [the longest x6 21.5 us: from_everyone(): return lax.all_to_all(copies, axis, split_axis=0, concat_axis=0, tiled=True)]
    all_gather x0 -> x2, blocking collectives: none -> 33.3 us  [the longest x1 19.7 us: on_device(): packed = jnp.swapaxes(lax.all_gather(packed, 'expert'), 0, 1)]
  transfers between devices with their start and end apart: 21 -> 0, of which waited for: 18 -> 0; matrix products, arithmetic and copies ran while one was open for 2% -> 0% of each run, Pallas kernels for 0% -> 0%
where the time goes in v1:
time: 300 us
  Pallas kernels  242 us (81%)
  blocking collectives  46.8 us (16%)
  local copies, waits for them, and re-layouts  5.43 us (2%)
  other arithmetic  3.89 us (1%)
    pallas_call x1, Pallas kernels, on_device(): pl.pallas_call(functools.partial(kernel, sections, n, (micros, T, Q, F, c...  242 us
    all_gather x1, blocking collectives, on_device(): packed = jnp.swapaxes(lax.all_gather(packed, 'expert'), 0, 1)  19.7 us
    all_gather x1, blocking collectives, on_device(): router_all = lax.all_gather(router, 'tensor', axis=0, tiled=True)  13.6 us
    psum x1, blocking collectives, on_device(): lax.psum(jnp.dot(normed, router, preferred_element_type=jnp.float32), 'te...  7.06 us
    psum x1, blocking collectives, on_device(): squares = lax.psum(jnp.sum(values * values, axis=-1), 'tensor')  6.4 us

profile of v1, /device:TPU:1, one launch (start us, length us, event | category | flops | bytes accessed | tf_op | source)
XLA Modules:
  0.0 299.8 jit_solution(16970921255157095607)
XLA Ops:
  0.0 1.1 multiply_reduce_fusion
  1.1 6.4 %psum.14 = f32[2,80]{1,0:T(2,128)S(1)} all-reduce(f32[2,80]{1,0:T(2,128)S(1)} %multiply_reduce_fusion), channel_id=1, replica_groups=mesh['section'=2,'expert'=16,'tensor'=4] {'tensor'}, use_global_device_ids=true, to_apply=%region_1.2 | all-reduce | flops 160 | bytes 1280 | tf_op jit(solution)/shard_map/psum | solution.py:350
  7.5 0.7 convert_reduce_fusion
  8.2 1.2 fusion.2
  9.4 7.1 %psum.15 = f32[2,80,4]{1,2,0:T(4,128)S(1)} all-reduce(f32[2,80,4]{1,2,0:T(4,128)S(1)} %fusion.2), channel_id=1, replica_groups=mesh['section'=2,'expert'=16,'tensor'=4] {'tensor'}, use_global_device_ids=true, to_apply=%region_2.3 | all-reduce | flops 640 | bytes 5120 | tf_op jit(solution)/shard_map/psum | solution.py:353
  16.4 0.7 select_reduce_fusion
  17.1 0.7 bitcast_convert_fusion
  17.8 19.7 %all-gather = f32[32,80,3]{1,2,0:T(4,128)S(1)} all-gather(f32[2,80,3]{1,2,0:T(4,128)S(1)} %pad_maximum_fusion.1), channel_id=2, replica_groups=mesh['section'=2,'expert'=16,'tensor'=4] {'expert'}, dimensions={0}, use_global_device_ids=true | all-gather | bytes 32640 | tf_op jit(solution)/shard_map/all_gather | solution.py:359
  37.6 0.2 fusion
  37.9 0.0 copy-start.1
  37.9 0.5 copy.43
  38.4 0.0 copy-start
  38.4 1.2 pad.8.clone
  39.5 0.7 broadcast_in_dim.35.scale
  40.3 0.0 copy-done.1
  40.3 0.2 copy.40
  40.5 13.6 %all-gather.1 = bf16[1,3072,4]{2,1,0:T(8,128)(2,1)S(1)} all-gather(bf16[1,768,4]{2,1,0:T(8,128)(2,1)S(1)} %copy.40), channel_id=3, replica_groups=mesh['section'=2,'expert'=16,'tensor'=4] {'tensor'}, dimensions={1}, use_global_device_ids=true | all-gather | bytes 30720 | tf_op jit(solution)/shard_map/all_gather | solution.py:376
  54.1 1.2 pad.9.rp_h
  55.3 0.0 copy-done
  55.3 0.6 convert_element_type.34.gain
  55.9 242.2 %layer_back.1 = bf16[2,80,768]{2,1,0:T(8,128)(2,1)} custom-call(bf16[2,80,768]{2,1,0:T(8,128)(2,1)} %gout.1, bf16[2,80,768]{2,1,0:T(8,128)(2,1)} %bitcast.57, f32[2,80,128]{2,1,0:T(8,128)} %broadcast_in_dim.35.scale, f32[1,768]{1,0:T(1,128)} %convert_element_type.34.gain, f32[2,4,4,80,128]{4,3,2,1,0:T(8,128)} %bitcast.50, bf16[2,16,64,512]{3,2,1,0:T(8,128)(2,1)} %bitcast.55, ...), custom_call_target="tpu_custom_call" | custom-call | tf_op jit(solution)/shard_map/layer_back/pallas_call | solution.py:385
  298.1 1.7 copy.47
  (11 shorter events, 0.1 us)
Async XLA Ops:
  37.9 2.4 copy-start.1
  38.4 16.9 %copy-start = (bf16[1,768]{1,0:T(2,128)(2,1)S(1)}, bf16[1,768]{1,0:T(2,128)(2,1)}, u32[]{:S(2)}) copy-start(bf16[1,768]{1,0:T(2,128)(2,1)} %param.12) | copy-start | bytes 4612

commit v2 on v1

--- a/solution.py
+++ b/solution.py
@@ -14,13 +14,14 @@
 
 def kernel(
     sections, n, sizes,
-    gout, xin, scale, gain, info_h, sg_h, su_h, wd_h, wg_h, wu_h, rp_h,
+    gout, xin, gain, rt_in, rows_in, sg_h, su_h, wd_h, wg_h, wu_h, rp_h,
     out,
     G, U, D, RH, RF, RHF, RFF, RX, hop, mrecv, msend,
     V, A, B, bt, DC, wd, wc, info, sg, su,
+    xo, gain_o, ps, pr, tot, GI, tmp,
     ld, x_s, x_r, fo_s, fo_r, ff_s, ff_r, so_s, so_r, sf_s, sf_r, dd_s, dd_r,
     e_s, e_r, rh_s, rh_r, rf_s, rf_r, hf_s, hf_r, ff2_s, ff2_r, rx_s, rx_r,
-    m_s, m_r, hop_s, hop_r, gate,
+    m_s, m_r, hop_s, hop_r, xo_s, xo_r, go_s, go_r, rp_s, rp_r, ps_s, ps_r, y_s, y_r, z_s, z_r, gate,
 ):
     micros, T, Q, F, cap, lanes = sizes
     width = 4 * Q
@@ -44,8 +45,11 @@
     xdiag = {"tensor": (1 - xl) * 2 + 1 - c}
     fdir = ({"expert": exid(at(fp, 1), sp)}, {"expert": exid(at(fp, -1), sp)})
     sdir = ({"expert": exid(fp, at(sp, 1))}, {"expert": exid(fp, at(sp, -1))})
+    across = (partner, xnbr, xdiag)
+    ypeer = tuple({"expert": z * n + at(y, o)} for o in (1, 2, 3))
+    zpeer = tuple({"expert": at(z, o) * n + y} for o in (1, 2, 3))
     hoppeer = {"section": 1 - sec, "tensor": (1 - xl) * 2 + c}
-    near = (partner, xnbr, xdiag) + fdir + sdir
+    near = across + fdir + sdir
 
     def load(k, src, dst):
         return pltpu.make_async_copy(src, dst, ld.at[k])
@@ -55,14 +59,14 @@
             load(0, wd_h, wd),
             load(1, wg_h, wc.at[:, pl.ds(0, F)]),
             load(2, wu_h, wc.at[:, pl.ds(F, F)]),
-            load(3, rp_h, wc.at[:, pl.ds(2 * F, lanes)]),
+            load(3, rp_h, wc.at[pl.ds(pl.multiple_of(te * Q, Q), Q), pl.ds(2 * F, lanes)]),
         )
 
     for cp in weight_loads():
         cp.start()
 
     barrier = pltpu.get_barrier_semaphore()
-    greeted = near + ((hoppeer,) if sections == 2 else ())
+    greeted = across + ypeer + zpeer + ((hoppeer,) if sections == 2 else ())
     for peer in greeted:
         pl.semaphore_signal(barrier, inc=1, device_id=peer, device_id_type=MESH)
     pl.semaphore_wait(barrier, len(greeted))
@@ -72,7 +76,113 @@
             src_ref=src, dst_ref=dst, send_sem=ss, recv_sem=rs, device_id=peer, device_id_type=MESH
         )
 
+    def send(src, dst, ss, rs, peer):
+        rc(src, dst, ss, rs, peer).start()
+
+    def arrived(ref, ss, rs, peer):
+        rc(ref, ref, ss, rs, peer).wait_recv()
+
+    def tensor_parts():
+        ps[...] = jnp.zeros_like(ps)
+        gr = rt_in[...].astype(jnp.float32) * gain[...]
+        hi = gr.astype(jnp.bfloat16)
+        lo = (gr - hi.astype(jnp.float32)).astype(jnp.bfloat16)
+        ones = jnp.ones((16, Q), jnp.bfloat16)
+        row = lax.broadcasted_iota(jnp.int32, (8, T), 0)
+
+        def nt(a, b):
+            return lax.dot_general(a, b, NT, preferred_element_type=jnp.float32)
+
+        for m in range(micros):
+            x = xin[m]
+            sq = x.astype(jnp.float32) * x.astype(jnp.float32)
+            h = sq.astype(jnp.bfloat16)
+            low = (sq - h.astype(jnp.float32)).astype(jnp.bfloat16)
+            logit = nt(hi, x) + nt(lo, x)
+            total = nt(ones, h) + nt(ones, low)
+            ps[m, :, 0:T] = jnp.where(row == 4, total[0:8], logit[0:8])
+        for i, peer in enumerate(across):
+            send(ps, pr.at[i], ps_s.at[i], ps_r.at[i], peer)
+
+    def spread_inputs():
+        send(xin, xo, xo_s, xo_r, xnbr)
+        send(gain, gain_o, go_s, go_r, xnbr)
+        for i, peer in enumerate(across):
+            place = wc.at[pl.ds(pl.multiple_of(te * Q, Q), Q), pl.ds(2 * F, lanes)]
+            send(rp_h, place, rp_s.at[i], rp_r.at[i], peer)
+
+    def route_rows():
+        for i, peer in enumerate(across):
+            arrived(pr.at[i], ps_s.at[i], ps_r.at[i], peer)
+        for m in range(micros):
+            tot[m] = (ps[m] + pr[0, m]) + (pr[1, m] + pr[2, m])
+            sc = lax.rsqrt(tot[m, 4:5] / width + norm_eps)
+            e0, e1 = rows_in[m, 0:1], rows_in[m, 1:2]
+            delta = jnp.zeros_like(sc)
+            for k in range(4):
+                pick = jnp.where(e0 == k, 1.0, 0.0) - jnp.where(e1 == k, 1.0, 0.0)
+                delta = delta + pick * (tot[m, k : k + 1] * sc)
+            GI[z, y, m, 0:1] = e0
+            GI[z, y, m, 1:2] = e1
+            GI[z, y, m, 2:3] = delta
+            GI[z, y, m, 3:4] = sc
+        for i, peer in enumerate(ypeer):
+            send(GI.at[z, y], GI.at[z, y], y_s.at[i], y_r.at[i], peer)
+
+    def rows_along_y():
+        for i in range(3):
+            arrived(GI.at[z, at(y, -1 - i)], y_s.at[i], y_r.at[i], ypeer[i])
+        for i, peer in enumerate(zpeer):
+            send(GI.at[z], GI.at[z], z_s.at[i], z_r.at[i], peer)
+
+    def rows_along_z():
+        for i in range(3):
+            arrived(GI.at[at(z, -1 - i)], z_s.at[i], z_r.at[i], zpeer[i])
+        own = z.astype(jnp.float32)
+        before = lax.broadcasted_iota(jnp.int32, (lanes, lanes), 0) < lax.broadcasted_iota(
+            jnp.int32, (lanes, lanes), 1
+        )
+        before = jnp.where(before, 1.0, 0.0).astype(jnp.bfloat16)
+        for m in range(micros):
+            for j in range(n * n):
+                for r in range(4):
+                    tmp[r, j : j + 1] = GI[j // n, j % n, m, r : r + 1]
+            e0, e1, delta = tmp[0], tmp[1], tmp[2]
+            is0 = jnp.where(e0 == own, 1.0, 0.0)
+            is1 = jnp.where(e1 == own, 1.0, 0.0)
+            used = is0 + is1
+            pos = jnp.dot(used.astype(jnp.bfloat16), before, preferred_element_type=jnp.float32)
+            pos = jnp.where(used > 0.5, pos, -1.0)
+            q0, q1 = jax.nn.sigmoid(delta), jax.nn.sigmoid(-delta)
+            parts = [pos, is0 * q0 + is1 * q1, is0 * q1 - is1 * q0]
+            for k in range(4):
+                parts.append(jnp.where(e0 == k, 1.0, 0.0) - jnp.where(e1 == k, 1.0, 0.0))
+            parts.append(tmp[3])
+            turned = jnp.concatenate(parts, axis=0).T[0:T]
+            for j in range(n * n):
+                info[m, j // n, j % n] = pltpu.roll(turned, (lanes - j) % lanes, 1)
+
+    def finish_prologue():
+        arrived(xo, xo_s, xo_r, xnbr)
+        arrived(gain_o, go_s, go_r, xnbr)
+        for i, o in enumerate((xl * 2 + 1 - c, (1 - xl) * 2 + c, (1 - xl) * 2 + 1 - c)):
+            place = wc.at[pl.ds(pl.multiple_of(o * Q, Q), Q), pl.ds(2 * F, lanes)]
+            arrived(place, rp_s.at[i], rp_r.at[i], across[i])
+        rc(xin, xo, xo_s, xo_r, xnbr).wait_send()
+        rc(gain, gain_o, go_s, go_r, xnbr).wait_send()
+        for i, peer in enumerate(across):
+            place = wc.at[pl.ds(pl.multiple_of(te * Q, Q), Q), pl.ds(2 * F, lanes)]
+            rc(rp_h, place, rp_s.at[i], rp_r.at[i], peer).wait_send()
+            rc(ps, pr.at[i], ps_s.at[i], ps_r.at[i], peer).wait_send()
+        for i, peer in enumerate(ypeer):
+            rc(GI.at[z, y], GI.at[z, y], y_s.at[i], y_r.at[i], peer).wait_send()
+        for i, peer in enumerate(zpeer):
+            rc(GI.at[z], GI.at[z], z_s.at[i], z_r.at[i], peer).wait_send()
+
     def one_micro(m, carry):
+        def first(f):
+            pl.when(m == 0)(f)
+
         @pl.when(m > 0)
         def _():
             for peer in near:
@@ -80,9 +190,8 @@
             pl.semaphore_wait(gate, len(near))
 
         small = (
-            load(4, info_h.at[m], info),
-            load(5, sg_h.at[m], sg),
-            load(6, su_h.at[m], su),
+            load(4, sg_h.at[m], sg),
+            load(5, su_h.at[m], su),
         )
         for cp in small:
             cp.start()
@@ -115,6 +224,7 @@
         go(mine.at[qh], mine.at[qh], x_s, x_r, xnbr)
         for d in range(2):
             go(mine.at[qh], mine.at[qh], fo_s.at[0, d], fo_r.at[0, d], fdir[d])
+        first(tensor_parts)
         V[...] = jnp.zeros_like(V)
         got(mine.at[qo], x_s, x_r, xnbr)
         for d in range(2):
@@ -129,17 +239,19 @@
 
         spread(0, mine)
         share(0, 0, mine)
+        first(spread_inputs)
+        first(route_rows)
         for cp in small:
             cp.wait()
 
-        @pl.when(m == 0)
+        @first
         def _():
             for cp in weight_loads():
                 cp.wait()
 
         def prepare(j, carry):
             i0, i1 = j // n, j % n
-            pos = info[i0, i1, :, 0:1]
+            pos = info[m, i0, i1, :, 0:1]
             slots = lax.broadcasted_iota(jnp.int32, (T, cap), 1).astype(jnp.float32)
             place = jnp.where(slots == pos, 1.0, 0.0).astype(jnp.bfloat16)
             a = jnp.dot(place, sg[j], preferred_element_type=jnp.float32)
@@ -170,7 +282,6 @@
                 else:
                     V[:, yi] += part
 
-        prepare_rows(0)
         for d in range(2):
             f = at(fp, -1 if d == 0 else 1)
             slot = G.at[c, sp, f]
@@ -179,6 +290,7 @@
             go(slot.at[d], slot.at[d], ff_s.at[d], ff_r.at[d], fdir[d])
             spread(1 + d, slot)
             share(0, 1 + d, slot)
+        first(rows_along_y)
         far = G.at[c, sp, at(fp, 2)]
         for d in range(2):
             got(far.at[d], ff_s.at[d], ff_r.at[d], fdir[d])
@@ -193,14 +305,17 @@
                 go(slot.at[d], slot.at[d], sf_s.at[k, d], sf_r.at[k, d], sdir[d])
                 share(1 + d, k, slot)
 
+        first(rows_along_z)
         pass_on(0)
-        prepare_rows(1)
+        prepare_rows(0)
         pass_on(1)
         into_v(0)
+        prepare_rows(1)
         pass_on(2)
         prepare_rows(2)
         pass_on(3)
         prepare_rows(3)
+        first(finish_prologue)
         for k in range(n):
             slot = G.at[c, at(sp, 2), at(fp, OFF[k])]
             for d in range(2):
@@ -217,10 +332,10 @@
             v = V[i0, i1]
             db = v * B[i0, i1]
             w = jnp.sum(db * bt[i0, i1].astype(jnp.float32), axis=-1, keepdims=True)
-            row = info[i0, i1]
+            row = info[m, i0, i1]
             DC[i0, i1, :, 0:F] = (v * A[i0, i1]).astype(jnp.bfloat16)
             DC[i0, i1, :, F : 2 * F] = db.astype(jnp.bfloat16)
-            DC[i0, i1, :, 2 * F :] = (w * row[:, 2:3] * row).astype(jnp.bfloat16)
+            DC[i0, i1, :, 2 * F :] = (w * row[:, 32:33] * row).astype(jnp.bfloat16)
             return carry
 
         lax.fori_loop(0, n * n, finish, 0)
@@ -229,7 +344,7 @@
             zi, yi = at(z, OFF[kk]), at(y, OFF[kk])
             for h in range(2):
                 da = (DC[zi] if h == 0 else DC[:, yi]).reshape(n * T, K)
-                q_own = (info[zi, :, :, 1:2] if h == 0 else info[:, yi, :, 1:2]).reshape(n * T, 1)
+                q_own = (info[m, zi, :, :, 16:17] if h == 0 else info[m, :, yi, :, 16:17]).reshape(n * T, 1)
 
                 def half(q, carry):
                     low = pl.multiple_of((2 * q + h) * Q, Q)
@@ -292,22 +407,22 @@
             total = U[c, sp, fp, q].astype(jnp.float32) + RFF[0, q].astype(jnp.float32)
             return total + RFF[1, q].astype(jnp.float32)
 
-        U[c, sp, fp, 1 - xl] = three(1 - xl).astype(jnp.bfloat16)
+        other = three(1 - xl)
+        U[c, sp, fp, 1 - xl] = other.astype(jnp.bfloat16)
         go(U.at[c, sp, fp, 1 - xl], RX, rx_s, rx_r, xnbr)
         dn = three(xl)
+
+        values = xin[m].astype(jnp.float32)
+        both = values * (dn * gain[...]) + xo[m].astype(jnp.float32) * (other * gain_o[...])
+        msend[...] = jnp.broadcast_to(jnp.sum(both, axis=-1, keepdims=True), msend.shape)
+        for i, peer in enumerate(across):
+            go(msend, mrecv.at[i], m_s.at[i], m_r.at[i], peer)
         got(RX, rx_s, rx_r, xnbr)
-        dn = dn + RX[...].astype(jnp.float32)
-
-        gained = dn * gain[...]
-        values = xin[m].astype(jnp.float32)
-        part = jnp.sum(values * gained, axis=-1, keepdims=True)
-        msend[...] = jnp.broadcast_to(part, msend.shape)
-        for i, peer in enumerate((partner, xnbr, xdiag)):
-            go(msend, mrecv.at[i], m_s.at[i], m_r.at[i], peer)
-        for i, peer in enumerate((partner, xnbr, xdiag)):
+        gained = (dn + RX[...].astype(jnp.float32)) * gain[...]
+        for i, peer in enumerate(across):
             got(mrecv.at[i], m_s.at[i], m_r.at[i], peer)
         moment = (msend[...] + mrecv[0] + mrecv[1] + mrecv[2])[:, 0:1] / width
-        sc = scale[m][:, 0:1]
+        sc = info[m, z, y, :, 112:113]
         result = G[c, sp, fp, xl].astype(jnp.float32) + sc * gained - values * (sc * sc * sc * moment)
         out[m] = result.astype(jnp.bfloat16)
         if sections == 2:
@@ -333,7 +448,6 @@
     layer_inputs, grad_out, norm_gain, router_w, w_gate, w_up, w_down, saved_gate, saved_up, routes
 ):
     sections = lax.axis_size("section")
-    holders = lax.axis_size("expert")
     n = 4
     micros, T, Q = grad_out.shape
     F = w_gate.shape[2]
@@ -342,40 +456,12 @@
     router = router_w[0]
     experts = router.shape[1]
     width = w_gate.shape[1]
-    own = lax.axis_index("expert") // (holders // experts)
     gain_full = norm_gain.astype(jnp.float32)
-    expert_ids = jnp.arange(experts, dtype=jnp.int32)
-
-    values = layer_inputs[0].astype(jnp.float32)
-    squares = lax.psum(jnp.sum(values * values, axis=-1), "tensor")
-    scale = lax.rsqrt(squares / width + norm_eps)[:, :, None]
-    normed = (values * scale * gain_full).astype(jnp.bfloat16)
-    logits = lax.psum(jnp.dot(normed, router, preferred_element_type=jnp.float32), "tensor")
-    chosen = routes[0]
-    onehot = (chosen[..., None] == expert_ids).astype(jnp.float32)
-    picked = jnp.sum(onehot * logits[:, :, None, :], axis=-1)
-    delta = picked[..., 0] - picked[..., 1]
-    packed = jnp.concatenate([chosen.astype(jnp.float32), delta[..., None]], axis=-1)
-    packed = jnp.swapaxes(lax.all_gather(packed, "expert"), 0, 1)
-    named = packed[..., :2].astype(jnp.int32)
-    q0, q1 = jax.nn.sigmoid(packed[..., 2]), jax.nn.sigmoid(-packed[..., 2])
-    is0, is1 = named[..., 0] == own, named[..., 1] == own
-    used = jnp.logical_or(is0, is1)
-    count = used.astype(jnp.float32)
-    earlier = jnp.tril(jnp.ones((T, T), jnp.float32), -1)
-    pos = jnp.einsum("mbt,ut->mbu", count, earlier)
-    pos = jnp.where(used, pos, -1.0)
-    q_own = jnp.where(is0, q0, jnp.where(is1, q1, 0.0))
-    q_other = jnp.where(is0, q1, jnp.where(is1, -q0, 0.0))
-    sign = (named[..., 0:1] == expert_ids).astype(jnp.float32) - (
-        named[..., 1:2] == expert_ids
-    ).astype(jnp.float32)
-    info = jnp.concatenate([pos[..., None], q_own[..., None], q_other[..., None], sign], axis=-1)
-    info = jnp.pad(info, ((0, 0), (0, 0), (0, 0), (0, lanes - info.shape[-1])))
-    info = info.reshape(micros, n, n, T, lanes)
-    router_all = lax.all_gather(router, "tensor", axis=0, tiled=True)
-    rp = jnp.pad(router_all, ((0, 0), (3, lanes - 3 - experts)))
-    scale_wide = jnp.broadcast_to(scale, (micros, T, lanes))
+    turned = jnp.pad(router.T, ((0, 16 - experts), (0, 0)))
+    rows = jnp.swapaxes(routes[0], 1, 2).astype(jnp.float32)
+    rows = jnp.pad(rows, ((0, 0), (0, 6), (0, lanes - T)), constant_values=-5.0)
+    spaced = jnp.pad(router[:, :, None], ((0, 0), (0, 0), (0, 15))).reshape(Q, experts * 16)
+    rp = jnp.pad(spaced, ((0, 0), (48, lanes - 48 - experts * 16)))
 
     bf, f32 = jnp.bfloat16, jnp.float32
     vm = pl.BlockSpec(memory_space=pltpu.VMEM)
@@ -385,7 +471,7 @@
     grads = pl.pallas_call(
         functools.partial(kernel, sections, n, (micros, T, Q, F, cap, lanes)),
         out_shape=jax.ShapeDtypeStruct((micros, T, Q), bf),
-        in_specs=[vm] * 4 + [anym] * 7,
+        in_specs=[vm] * 5 + [anym] * 6,
         out_specs=vm,
         scratch_shapes=[
             pltpu.VMEM((2, n, n, 2, T, Q), bf),
@@ -406,10 +492,17 @@
             pltpu.VMEM((n, n, T, K), bf),
             pltpu.VMEM((F, width), bf),
             pltpu.VMEM((width, K), bf),
-            pltpu.VMEM((n, n, T, lanes), f32),
+            pltpu.VMEM((micros, n, n, T, lanes), f32),
             pltpu.VMEM((n * n, cap, F), bf),
             pltpu.VMEM((n * n, cap, F), bf),
-            dma((7,)),
+            pltpu.VMEM((micros, T, Q), bf),
+            pltpu.VMEM((1, Q), f32),
+            pltpu.VMEM((micros, 8, lanes), f32),
+            pltpu.VMEM((3, micros, 8, lanes), f32),
+            pltpu.VMEM((micros, 8, lanes), f32),
+            pltpu.VMEM((n, n, micros, 8, lanes), f32),
+            pltpu.VMEM((4, n * n, lanes), f32),
+            dma((6,)),
             dma, dma,
             dma((2, 2)), dma((2, 2)), dma((2,)), dma((2,)),
             dma((4, 2)), dma((4, 2)), dma((4, 2)), dma((4, 2)),
@@ -417,6 +510,8 @@
             dma((4,)), dma((4,)), dma((2,)), dma((2,)), dma((2, 4)), dma((2, 4)),
             dma((2,)), dma((2,)), dma((2,)), dma((2,)), dma, dma,
             dma((3,)), dma((3,)), dma((micros,)), dma((micros,)),
+            dma, dma, dma, dma, dma((3,)), dma((3,)), dma((3,)), dma((3,)),
+            dma((3,)), dma((3,)), dma((3,)), dma((3,)),
             pltpu.SemaphoreType.REGULAR,
         ],
         compiler_params=pltpu.CompilerParams(
@@ -424,7 +519,7 @@
         ),
         name="layer_back",
     )(
-        grad_out, layer_inputs[0], scale_wide, gain_full, info, saved_gate[0], saved_up[0],
+        grad_out, layer_inputs[0], gain_full, turned, rows, saved_gate[0], saved_up[0],
         w_down[0], w_gate[0], w_up[0], rp,
     )
     return grads[None]

time: 300 us -> 252 us (0.84)
  blocking collectives: 46.8 us -> 0 us
    all_gather x2 -> x0, blocking collectives: 33.3 us -> none  [the longest x1 19.7 us: on_device(): packed = jnp.swapaxes(lax.all_gather(packed, 'expert'), 0, 1)]
    psum x2 -> x0, blocking collectives: 13.5 us -> none  [the longest x1 7.06 us: on_device(): lax.psum(jnp.dot(normed, router, preferred_element_type=jnp.float32), 'te...]
where the time goes in v2:
time: 252 us; the launch traced here: 251 us
  Pallas kernels  244 us (97%)
  local copies, waits for them, and re-layouts  5.25 us (2%)
    pallas_call x1, Pallas kernels, on_device(): pl.pallas_call(functools.partial(kernel, sections, n, (micros, T, Q, F, c...  244 us

profile of v2, /device:TPU:1, one launch (start us, length us, event | category | flops | bytes accessed | tf_op | source)
XLA Modules:
  0.0 251.3 jit_solution(10236969659808457919)
XLA Ops:
  0.0 0.7 convert_bitcast_fusion
  0.7 1.3 convert_element_type.18.gain
  2.0 0.6 pad.17.rows_in
  2.6 0.7 copy.15
  3.3 1.3 pad.16.rt_in
  4.6 0.2 copy.14
  4.8 0.8 pad.19.rp_h
  5.6 244.1 %layer_back.1 = bf16[2,80,768]{2,1,0:T(8,128)(2,1)} custom-call(bf16[2,80,768]{2,1,0:T(8,128)(2,1)} %gout.1, bf16[2,80,768]{2,1,0:T(8,128)(2,1)} %bitcast.23, f32[1,768]{1,0:T(1,128)} %convert_element_type.18.gain, bf16[16,768]{1,0:T(8,128)(2,1)} %pad.16.rt_in, f32[2,8,128]{2,1,0:T(8,128)} %pad.17.rows_in, bf16[2,16,64,512]{3,2,1,0:T(8,128)(2,1)} %bitcast.19, ...), custom_call_target="tpu_custom_call" | custom-call | tf_op jit(solution)/shard_map/layer_back/pallas_call | solution.py:471
  249.7 1.7 copy.17
  (1 shorter events, 0.0 us)

commit v3 on v2

--- a/solution.py
+++ b/solution.py
@@ -19,7 +19,7 @@
     G, U, D, RH, RF, RHF, RFF, RX, hop, mrecv, msend,
     V, A, B, bt, DC, wd, wc, info, sg, su,
     xo, gain_o, ps, pr, tot, GI, tmp,
-    ld, x_s, x_r, fo_s, fo_r, ff_s, ff_r, so_s, so_r, sf_s, sf_r, dd_s, dd_r,
+    ld, x_s, x_r, fo_s, fo_r, ff_s, ff_r, sq_s, sq_r, so_s, so_r, sf_s, sf_r, dd_s, dd_r,
     e_s, e_r, rh_s, rh_r, rf_s, rf_r, hf_s, hf_r, ff2_s, ff2_r, rx_s, rx_r,
     m_s, m_r, hop_s, hop_r, xo_s, xo_r, go_s, go_r, rp_s, rp_r, ps_s, ps_r, y_s, y_r, z_s, z_r, gate,
 ):
@@ -180,9 +180,6 @@
             rc(GI.at[z], GI.at[z], z_s.at[i], z_r.at[i], peer).wait_send()
 
     def one_micro(m, carry):
-        def first(f):
-            pl.when(m == 0)(f)
-
         @pl.when(m > 0)
         def _():
             for peer in near:
@@ -206,48 +203,10 @@
             rc(ref, ref, ss, rs, peer).wait_recv()
 
         top = sec == sections - 1
-        qh = jnp.where(top, xl, 1 - xl)
-        qo = 1 - qh
-        mine = G.at[c, sp, fp]
-
-        @pl.when(top)
-        def _():
-            G[c, sp, fp, qh] = gout[m]
-
-        if sections == 2:
-
-            @pl.when(jnp.logical_not(top))
-            def _():
-                got(hop.at[m], hop_s.at[m], hop_r.at[m], hoppeer)
-                G[c, sp, fp, qh] = hop[m]
-
-        go(mine.at[qh], mine.at[qh], x_s, x_r, xnbr)
-        for d in range(2):
-            go(mine.at[qh], mine.at[qh], fo_s.at[0, d], fo_r.at[0, d], fdir[d])
-        first(tensor_parts)
-        V[...] = jnp.zeros_like(V)
-        got(mine.at[qo], x_s, x_r, xnbr)
-        for d in range(2):
-            go(mine.at[qo], mine.at[qo], fo_s.at[1, d], fo_r.at[1, d], fdir[d])
-
-        def spread(k, slot):
-            for d in range(2):
-                go(slot, slot, so_s.at[k, d], so_r.at[k, d], sdir[d])
-
-        def share(kk, k, slot):
-            go(slot, slot, dd_s.at[kk, k], dd_r.at[kk, k], partner)
-
-        spread(0, mine)
-        share(0, 0, mine)
-        first(spread_inputs)
-        first(route_rows)
-        for cp in small:
-            cp.wait()
-
-        @first
-        def _():
-            for cp in weight_loads():
-                cp.wait()
+        ahead = jnp.logical_and(m == 0, jnp.logical_not(top))
+
+        def first(f):
+            pl.when(jnp.logical_and(m == 0, top))(f)
 
         def prepare(j, carry):
             i0, i1 = j // n, j % n
@@ -263,7 +222,74 @@
             return carry
 
         def prepare_rows(i):
-            lax.fori_loop(i * n, (i + 1) * n, prepare, 0)
+            @pl.when(jnp.logical_not(ahead))
+            def _():
+                lax.fori_loop(i * n, (i + 1) * n, prepare, 0)
+
+        if sections == 2:
+
+            @pl.when(ahead)
+            def _():
+                tensor_parts()
+                spread_inputs()
+                route_rows()
+                rows_along_y()
+                rows_along_z()
+                for cp in small:
+                    cp.wait()
+                for cp in weight_loads():
+                    cp.wait()
+                finish_prologue()
+                lax.fori_loop(0, n * n, prepare, 0)
+
+        qh = jnp.where(top, xl, 1 - xl)
+        qo = 1 - qh
+        mine = G.at[c, sp, fp]
+
+        @pl.when(top)
+        def _():
+            G[c, sp, fp, qh] = gout[m]
+
+        if sections == 2:
+
+            @pl.when(jnp.logical_not(top))
+            def _():
+                got(hop.at[m], hop_s.at[m], hop_r.at[m], hoppeer)
+                G[c, sp, fp, qh] = hop[m]
+
+        go(mine.at[qh], mine.at[qh], x_s, x_r, xnbr)
+        for d in range(2):
+            go(mine.at[qh], mine.at[qh], fo_s.at[0, d], fo_r.at[0, d], fdir[d])
+        for d in range(2):
+            go(mine.at[qh], mine.at[qh], sq_s.at[0, d], sq_r.at[0, d], sdir[d])
+        first(tensor_parts)
+        V[...] = jnp.zeros_like(V)
+        got(mine.at[qo], x_s, x_r, xnbr)
+        for d in range(2):
+            go(mine.at[qo], mine.at[qo], fo_s.at[1, d], fo_r.at[1, d], fdir[d])
+        for d in range(2):
+            go(mine.at[qo], mine.at[qo], sq_s.at[1, d], sq_r.at[1, d], sdir[d])
+
+        def spread(k, slot):
+            for d in range(2):
+                go(slot, slot, so_s.at[k, d], so_r.at[k, d], sdir[d])
+
+        def share(kk, k, slot):
+            go(slot, slot, dd_s.at[kk, k], dd_r.at[kk, k], partner)
+
+        share(0, 0, mine)
+        first(spread_inputs)
+        first(route_rows)
+
+        @pl.when(jnp.logical_not(ahead))
+        def _():
+            for cp in small:
+                cp.wait()
+
+        @first
+        def _():
+            for cp in weight_loads():
+                cp.wait()
 
         def into_v(kk):
             for k in range(n):
@@ -301,7 +327,11 @@
             f = at(fp, OFF[k])
             for d in range(2):
                 slot = G.at[c, at(sp, -1 if d == 0 else 1), f]
-                got(slot, so_s.at[k, d], so_r.at[k, d], sdir[d])
+                if k == 0:
+                    for i, q in enumerate((qh, qo)):
+                        got(slot.at[q], sq_s.at[i, d], sq_r.at[i, d], sdir[d])
+                else:
+                    got(slot, so_s.at[k, d], so_r.at[k, d], sdir[d])
                 go(slot.at[d], slot.at[d], sf_s.at[k, d], sf_r.at[k, d], sdir[d])
                 share(1 + d, k, slot)
 
@@ -325,10 +355,8 @@
                 into_v(1)
             if k == 2:
                 into_v(2)
-        into_v(3)
-
-        def finish(j, carry):
-            i0, i1 = j // n, j % n
+
+        def finish(i0, i1):
             v = V[i0, i1]
             db = v * B[i0, i1]
             w = jnp.sum(db * bt[i0, i1].astype(jnp.float32), axis=-1, keepdims=True)
@@ -336,51 +364,86 @@
             DC[i0, i1, :, 0:F] = (v * A[i0, i1]).astype(jnp.bfloat16)
             DC[i0, i1, :, F : 2 * F] = db.astype(jnp.bfloat16)
             DC[i0, i1, :, 2 * F :] = (w * row[:, 32:33] * row).astype(jnp.bfloat16)
+
+        def finish_near(j, carry):
+            i, k = j // 3, j % 3
+            finish(at(z, i + i // 2), at(y, k + k // 2))
             return carry
 
-        lax.fori_loop(0, n * n, finish, 0)
-
-        def into_u(kk):
+        def finish_far(j, carry):
+            k = j - 4
+            o = k + k // 2
+            finish(at(z, jnp.where(j < 4, 2, o)), at(y, jnp.where(j < 4, j, 2)))
+            return carry
+
+        lax.fori_loop(0, 9, finish_near, 0)
+        into_v(3)
+        lax.fori_loop(0, 7, finish_far, 0)
+
+        def half_u(kk, h, theirs):
             zi, yi = at(z, OFF[kk]), at(y, OFF[kk])
-            for h in range(2):
-                da = (DC[zi] if h == 0 else DC[:, yi]).reshape(n * T, K)
-                q_own = (info[m, zi, :, :, 16:17] if h == 0 else info[m, :, yi, :, 16:17]).reshape(n * T, 1)
-
-                def half(q, carry):
-                    low = pl.multiple_of((2 * q + h) * Q, Q)
-                    u = lax.dot_general(
-                        da, wc[pl.ds(low, Q), :], NT, preferred_element_type=jnp.float32
-                    )
-                    u = (u * q_own).astype(jnp.bfloat16).reshape(n, T, Q)
-                    U[h, zi if h == 0 else yi, :, q] = u
-                    return carry
-
-                lax.fori_loop(0, 2, half, 0)
-            go(U.at[1 - c, at(fp, OFF[kk])], D.at[kk], e_s.at[kk], e_r.at[kk], partner)
-
-        def add_partner(kk):
-            got(D.at[kk], e_s.at[kk], e_r.at[kk], partner)
+            da = (DC[zi] if h == 0 else DC[:, yi]).reshape(n * T, K)
+            q_own = (info[m, zi, :, :, 16:17] if h == 0 else info[m, :, yi, :, 16:17]).reshape(n * T, 1)
+            group = zi if h == 0 else yi
+
+            def quarter(q, carry):
+                low = pl.multiple_of((2 * q + h) * Q, Q)
+                u = lax.dot_general(da, wc[pl.ds(low, Q), :], NT, preferred_element_type=jnp.float32)
+                U[h, group, :, q] = (u * q_own).astype(jnp.bfloat16).reshape(n, T, Q)
+                if theirs:
+                    rc(U.at[h, group, :, q], D.at[kk, :, q], e_s.at[kk, q], e_r.at[kk, q], partner).start()
+                return carry
+
+            lax.fori_loop(0, 2, quarter, 0)
+
+        def u_for_partner(kk):
+            for core in range(2):
+                pl.when(c == core)(functools.partial(half_u, kk, 1 - core, True))
+            for q in range(2):
+                sent.append(
+                    rc(U.at[1 - c, at(fp, OFF[kk]), :, q], D.at[kk, :, q], e_s.at[kk, q], e_r.at[kk, q], partner)
+                )
+
+        def u_for_self(kk):
+            for core in range(2):
+                pl.when(c == core)(functools.partial(half_u, kk, core, False))
+
+        def add_partner(kk, q):
+            got(D.at[kk, :, q], e_s.at[kk, q], e_r.at[kk, q], partner)
             i = at(sp, OFF[kk])
-            U[c, i] = U[c, i] + D[kk]
-
-        into_u(3)
-        add_partner(3)
+            U[c, i, :, q] = U[c, i, :, q] + D[kk, :, q]
+
+        u_for_partner(3)
+        u_for_self(3)
+        u_for_partner(2)
         s2 = at(sp, 2)
         for d in range(2):
-            go(U.at[c, s2, :, d], RH.at[d], rh_s.at[d], rh_r.at[d], sdir[d])
-        into_u(2)
-        add_partner(2)
-        into_u(1)
-        add_partner(1)
-        for d in range(2):
-            i = at(sp, 1 if d == 0 else -1)
-            got(RH.at[d], rh_s.at[d], rh_r.at[d], sdir[d])
-            U[c, i, :, d] = U[c, i, :, d] + RH[d]
+            add_partner(3, d)
             for k in (3, 2, 1, 0):
-                f = at(fp, OFF[k])
+                go(U.at[c, s2, at(fp, OFF[k]), d], RH.at[d, k], rh_s.at[d, k], rh_r.at[d, k], sdir[d])
+        u_for_self(2)
+        u_for_partner(1)
+        u_for_self(1)
+        for q in range(2):
+            add_partner(2, q)
+        for q in range(2):
+            add_partner(1, q)
+
+        def pass_sum(k):
+            for d in range(2):
+                i, f = at(sp, 1 if d == 0 else -1), at(fp, OFF[k])
+                got(RH.at[d, k], rh_s.at[d, k], rh_r.at[d, k], sdir[d])
+                U[c, i, f, d] = U[c, i, f, d] + RH[d, k]
                 go(U.at[c, i, f], RF.at[d, k], rf_s.at[d, k], rf_r.at[d, k], sdir[d])
-        into_u(0)
-        add_partner(0)
+
+        pass_sum(3)
+        pass_sum(2)
+        u_for_partner(0)
+        pass_sum(1)
+        pass_sum(0)
+        u_for_self(0)
+        for q in range(2):
+            add_partner(0, q)
 
         def own_sum(k):
             for d in range(2):
@@ -398,19 +461,20 @@
             f = at(fp, OFF[k])
             got(RHF.at[d], hf_s.at[d], hf_r.at[d], fdir[d])
             U[c, sp, f, d] = U[c, sp, f, d] + RHF[d]
-            go(U.at[c, sp, f], RFF.at[d], ff2_s.at[d], ff2_r.at[d], fdir[d])
+            for i, q in enumerate((1 - xl, xl)):
+                go(U.at[c, sp, f, q], RFF.at[d, q], ff2_s.at[d, i], ff2_r.at[d, i], fdir[d])
         own_sum(0)
-        for d in range(2):
-            got(RFF.at[d], ff2_s.at[d], ff2_r.at[d], fdir[d])
-
-        def three(q):
+
+        def three(i, q):
+            for d in range(2):
+                got(RFF.at[d, q], ff2_s.at[d, i], ff2_r.at[d, i], fdir[d])
             total = U[c, sp, fp, q].astype(jnp.float32) + RFF[0, q].astype(jnp.float32)
             return total + RFF[1, q].astype(jnp.float32)
 
-        other = three(1 - xl)
+        other = three(0, 1 - xl)
         U[c, sp, fp, 1 - xl] = other.astype(jnp.bfloat16)
         go(U.at[c, sp, fp, 1 - xl], RX, rx_s, rx_r, xnbr)
-        dn = three(xl)
+        dn = three(1, xl)
 
         values = xin[m].astype(jnp.float32)
         both = values * (dn * gain[...]) + xo[m].astype(jnp.float32) * (other * gain_o[...])
@@ -505,10 +569,10 @@
             dma((6,)),
             dma, dma,
             dma((2, 2)), dma((2, 2)), dma((2,)), dma((2,)),
-            dma((4, 2)), dma((4, 2)), dma((4, 2)), dma((4, 2)),
+            dma((2, 2)), dma((2, 2)), dma((4, 2)), dma((4, 2)), dma((4, 2)), dma((4, 2)),
             dma((4, 4)), dma((4, 4)),
-            dma((4,)), dma((4,)), dma((2,)), dma((2,)), dma((2, 4)), dma((2, 4)),
-            dma((2,)), dma((2,)), dma((2,)), dma((2,)), dma, dma,
+            dma((4, 2)), dma((4, 2)), dma((2, 4)), dma((2, 4)), dma((2, 4)), dma((2, 4)),
+            dma((2,)), dma((2,)), dma((2, 2)), dma((2, 2)), dma, dma,
             dma((3,)), dma((3,)), dma((micros,)), dma((micros,)),
             dma, dma, dma, dma, dma((3,)), dma((3,)), dma((3,)), dma((3,)),
             dma((3,)), dma((3,)), dma((3,)), dma((3,)),

time: 252 us -> 224 us (0.89)
  Pallas kernels: 244 us -> 217 us
    pallas_call x1, Pallas kernels: 244 us -> 217 us  [on_device(): pl.pallas_call(functools.partial(kernel, sections, n, (micros, T, Q, F, c...]
where the time goes in v3:
time: 224 us
  Pallas kernels  217 us (97%)
  local copies, waits for them, and re-layouts  5.25 us (2%)
    pallas_call x1, Pallas kernels, on_device(): pl.pallas_call(functools.partial(kernel, sections, n, (micros, T, Q, F, c...  217 us

profile of v3, /device:TPU:1, one launch (start us, length us, event | category | flops | bytes accessed | tf_op | source)
XLA Modules:
  0.0 224.2 jit_solution(501088266628875778)
XLA Ops:
  0.0 0.7 convert_bitcast_fusion
  0.7 1.3 convert_element_type.18.gain
  2.0 0.6 pad.17.rows_in
  2.6 0.7 copy.15
  3.3 1.3 pad.16.rt_in
  4.6 0.2 copy.14
  4.8 0.8 pad.19.rp_h
  5.6 217.0 %layer_back.1 = bf16[2,80,768]{2,1,0:T(8,128)(2,1)} custom-call(bf16[2,80,768]{2,1,0:T(8,128)(2,1)} %gout.1, bf16[2,80,768]{2,1,0:T(8,128)(2,1)} %bitcast.23, f32[1,768]{1,0:T(1,128)} %convert_element_type.18.gain, bf16[16,768]{1,0:T(8,128)(2,1)} %pad.16.rt_in, f32[2,8,128]{2,1,0:T(8,128)} %pad.17.rows_in, bf16[2,16,64,512]{3,2,1,0:T(8,128)(2,1)} %bitcast.19, ...), custom_call_target="tpu_custom_call" | custom-call | tf_op jit(solution)/shard_map/layer_back/pallas_call | solution.py:535
  222.5 1.7 copy.17
  (1 shorter events, 0.0 us)

commit v4 on v3

--- a/solution.py
+++ b/solution.py
@@ -14,12 +14,12 @@
 
 def kernel(
     sections, n, sizes,
-    gout, xin, gain, rt_in, rows_in, sg_h, su_h, wd_h, wg_h, wu_h, rp_h,
+    gout, xin, gain_in, rt_in, rows_in, sg_h, su_h, wd_h, wg_h, wu_h,
     out,
     G, U, D, RH, RF, RHF, RFF, RX, hop, mrecv, msend,
     V, A, B, bt, DC, wd, wc, info, sg, su,
-    xo, gain_o, ps, pr, tot, GI, tmp,
-    ld, x_s, x_r, fo_s, fo_r, ff_s, ff_r, sq_s, sq_r, so_s, so_r, sf_s, sf_r, dd_s, dd_r,
+    xo, gain, gain_o, rp, ps, pr, tot, GI, tmp,
+    ld, x_s, x_r, fo_s, fo_r, ff_s, ff_r, so_s, so_r, sf_s, sf_r, dd_s, dd_r,
     e_s, e_r, rh_s, rh_r, rf_s, rf_r, hf_s, hf_r, ff2_s, ff2_r, rx_s, rx_r,
     m_s, m_r, hop_s, hop_r, xo_s, xo_r, go_s, go_r, rp_s, rp_r, ps_s, ps_r, y_s, y_r, z_s, z_r, gate,
 ):
@@ -59,7 +59,6 @@
             load(0, wd_h, wd),
             load(1, wg_h, wc.at[:, pl.ds(0, F)]),
             load(2, wu_h, wc.at[:, pl.ds(F, F)]),
-            load(3, rp_h, wc.at[pl.ds(pl.multiple_of(te * Q, Q), Q), pl.ds(2 * F, lanes)]),
         )
 
     for cp in weight_loads():
@@ -84,6 +83,15 @@
 
     def tensor_parts():
         ps[...] = jnp.zeros_like(ps)
+        gain[...] = gain_in[...].astype(jnp.float32)
+        at_lane = lax.broadcasted_iota(jnp.int32, (lanes, 16), 0)
+        spaced = at_lane == 48 + 16 * lax.broadcasted_iota(jnp.int32, (lanes, 16), 1)
+        spaced = jnp.where(spaced, 1.0, 0.0).astype(jnp.bfloat16)
+        router = lax.dot_general(
+            rt_in[...], spaced, (((0,), (1,)), ((), ())), preferred_element_type=jnp.float32
+        ).astype(jnp.bfloat16)
+        rp[...] = router
+        wc[pl.ds(pl.multiple_of(te * Q, Q), Q), 2 * F :] = router
         gr = rt_in[...].astype(jnp.float32) * gain[...]
         hi = gr.astype(jnp.bfloat16)
         lo = (gr - hi.astype(jnp.float32)).astype(jnp.bfloat16)
@@ -109,7 +117,7 @@
         send(gain, gain_o, go_s, go_r, xnbr)
         for i, peer in enumerate(across):
             place = wc.at[pl.ds(pl.multiple_of(te * Q, Q), Q), pl.ds(2 * F, lanes)]
-            send(rp_h, place, rp_s.at[i], rp_r.at[i], peer)
+            send(rp, place, rp_s.at[i], rp_r.at[i], peer)
 
     def route_rows():
         for i, peer in enumerate(across):
@@ -172,7 +180,7 @@
         rc(gain, gain_o, go_s, go_r, xnbr).wait_send()
         for i, peer in enumerate(across):
             place = wc.at[pl.ds(pl.multiple_of(te * Q, Q), Q), pl.ds(2 * F, lanes)]
-            rc(rp_h, place, rp_s.at[i], rp_r.at[i], peer).wait_send()
+            rc(rp, place, rp_s.at[i], rp_r.at[i], peer).wait_send()
             rc(ps, pr.at[i], ps_s.at[i], ps_r.at[i], peer).wait_send()
         for i, peer in enumerate(ypeer):
             rc(GI.at[z, y], GI.at[z, y], y_s.at[i], y_r.at[i], peer).wait_send()
@@ -260,19 +268,23 @@
         go(mine.at[qh], mine.at[qh], x_s, x_r, xnbr)
         for d in range(2):
             go(mine.at[qh], mine.at[qh], fo_s.at[0, d], fo_r.at[0, d], fdir[d])
-        for d in range(2):
-            go(mine.at[qh], mine.at[qh], sq_s.at[0, d], sq_r.at[0, d], sdir[d])
+        def spread(k, i, piece):
+            for d in range(2):
+                go(piece, piece, so_s.at[k, i, d], so_r.at[k, i, d], sdir[d])
+
+        def forward(piece, ss, rs, peer):
+            cp = rc(piece, piece, ss, rs, peer)
+            sent.append(cp)
+            return cp.start
+
+        spread(0, 0, mine.at[qh])
         first(tensor_parts)
         V[...] = jnp.zeros_like(V)
+        msend[...] = jnp.zeros_like(msend)
         got(mine.at[qo], x_s, x_r, xnbr)
         for d in range(2):
             go(mine.at[qo], mine.at[qo], fo_s.at[1, d], fo_r.at[1, d], fdir[d])
-        for d in range(2):
-            go(mine.at[qo], mine.at[qo], sq_s.at[1, d], sq_r.at[1, d], sdir[d])
-
-        def spread(k, slot):
-            for d in range(2):
-                go(slot, slot, so_s.at[k, d], so_r.at[k, d], sdir[d])
+        spread(0, 1, mine.at[qo])
 
         def share(kk, k, slot):
             go(slot, slot, dd_s.at[kk, k], dd_r.at[kk, k], partner)
@@ -291,49 +303,62 @@
             for cp in weight_loads():
                 cp.wait()
 
-        def into_v(kk):
+        def half_v(kk, h):
+            zi, yi = at(z, OFF[kk]), at(y, OFF[kk])
+            part = jnp.zeros((n * T, F), jnp.float32)
+            for q in range(2):
+                g = (G[0, zi, :, q] if h == 0 else G[1, yi, :, q]).reshape(n * T, Q)
+                w = wd[:, (2 * q + h) * Q : (2 * q + h + 1) * Q]
+                part = part + lax.dot_general(g, w, NT, preferred_element_type=jnp.float32)
+            part = part.reshape(n, T, F)
+            if h == 0:
+                V[zi] += part
+            else:
+                V[:, yi] += part
+
+        def v_shared(kk):
             for k in range(n):
                 ref = G.at[1 - c, at(fp, OFF[kk]), at(sp, OFF[k])]
                 got(ref, dd_s.at[kk, k], dd_r.at[kk, k], partner)
-            zi, yi = at(z, OFF[kk]), at(y, OFF[kk])
+
+        def into_v(kk):
+            v_shared(kk)
             for h in range(2):
-                part = jnp.zeros((n * T, F), jnp.float32)
-                for q in range(2):
-                    g = (G[0, zi, :, q] if h == 0 else G[1, yi, :, q]).reshape(n * T, Q)
-                    w = wd[:, (2 * q + h) * Q : (2 * q + h + 1) * Q]
-                    part = part + lax.dot_general(g, w, NT, preferred_element_type=jnp.float32)
-                part = part.reshape(n, T, F)
-                if h == 0:
-                    V[zi] += part
-                else:
-                    V[:, yi] += part
-
-        for d in range(2):
-            f = at(fp, -1 if d == 0 else 1)
-            slot = G.at[c, sp, f]
-            for i, q in enumerate((qh, qo)):
-                got(slot.at[q], fo_s.at[i, d], fo_r.at[i, d], fdir[d])
-            go(slot.at[d], slot.at[d], ff_s.at[d], ff_r.at[d], fdir[d])
-            spread(1 + d, slot)
-            share(0, 1 + d, slot)
+                half_v(kk, h)
+
+        fslot = tuple(G.at[c, sp, at(fp, o)] for o in (-1, 1))
+        fnext = [
+            forward(fslot[d].at[d], ff_s.at[d], ff_r.at[d], fdir[d]) for d in range(2)
+        ]
+        for i, q in enumerate((qh, qo)):
+            for d in range(2):
+                got(fslot[d].at[q], fo_s.at[i, d], fo_r.at[i, d], fdir[d])
+                pl.when(q == d)(fnext[d])
+                spread(1 + d, i, fslot[d].at[q])
+        for d in range(2):
+            share(0, 1 + d, fslot[d])
         first(rows_along_y)
         far = G.at[c, sp, at(fp, 2)]
         for d in range(2):
             got(far.at[d], ff_s.at[d], ff_r.at[d], fdir[d])
-        spread(3, far)
+            spread(3, d, far.at[d])
         share(0, 3, far)
 
         def pass_on(k):
             f = at(fp, OFF[k])
+            slots = tuple(G.at[c, at(sp, o), f] for o in (-1, 1))
+            nexts = [
+                forward(slots[d].at[d], sf_s.at[k, d], sf_r.at[k, d], sdir[d]) for d in range(2)
+            ]
+            for i, q in enumerate((qh, qo) if k < 3 else (0, 1)):
+                for d in range(2):
+                    got(slots[d].at[q], so_s.at[k, i, d], so_r.at[k, i, d], sdir[d])
+                    if k < 3:
+                        pl.when(q == d)(nexts[d])
+                    elif q == d:
+                        nexts[d]()
             for d in range(2):
-                slot = G.at[c, at(sp, -1 if d == 0 else 1), f]
-                if k == 0:
-                    for i, q in enumerate((qh, qo)):
-                        got(slot.at[q], sq_s.at[i, d], sq_r.at[i, d], sdir[d])
-                else:
-                    got(slot, so_s.at[k, d], so_r.at[k, d], sdir[d])
-                go(slot.at[d], slot.at[d], sf_s.at[k, d], sf_r.at[k, d], sdir[d])
-                share(1 + d, k, slot)
+                share(1 + d, k, slots[d])
 
         first(rows_along_z)
         pass_on(0)
@@ -371,99 +396,99 @@
             return carry
 
         def finish_far(j, carry):
-            k = j - 4
-            o = k + k // 2
-            finish(at(z, jnp.where(j < 4, 2, o)), at(y, jnp.where(j < 4, j, 2)))
+            o, p = ((2, 0), (2, 1), (2, 2), (2, 3), (0, 2), (1, 2), (3, 2))[j]
+            finish(at(z, o), at(y, p))
             return carry
 
         lax.fori_loop(0, 9, finish_near, 0)
-        into_v(3)
-        lax.fori_loop(0, 7, finish_far, 0)
-
-        def half_u(kk, h, theirs):
+        for core in range(2):
+            pl.when(c == core)(functools.partial(half_v, 3, core))
+        v_shared(3)
+        for core in range(2):
+            pl.when(c == core)(functools.partial(half_v, 3, 1 - core))
+        for j in range(7):
+            finish_far(j, 0)
+
+        def half_u(blocks, h, q):
+            da = jnp.concatenate([DC[i, k] for i, k in blocks], axis=0)
+            q_own = jnp.concatenate([info[m, i, k, :, 16:17] for i, k in blocks], axis=0)
+            w = wc[pl.ds(pl.multiple_of((2 * q + h) * Q, Q), Q), :]
+            u = lax.dot_general(da, w, NT, preferred_element_type=jnp.float32)
+            u = (u * q_own).astype(jnp.bfloat16)
+            for j, (i, k) in enumerate(blocks):
+                U[h, i * (1 - h) + k * h, k * (1 - h) + i * h, q] = u[j * T : (j + 1) * T]
+
+        def unit(kk, q):
             zi, yi = at(z, OFF[kk]), at(y, OFF[kk])
-            da = (DC[zi] if h == 0 else DC[:, yi]).reshape(n * T, K)
-            q_own = (info[m, zi, :, :, 16:17] if h == 0 else info[m, :, yi, :, 16:17]).reshape(n * T, 1)
-            group = zi if h == 0 else yi
-
-            def quarter(q, carry):
-                low = pl.multiple_of((2 * q + h) * Q, Q)
-                u = lax.dot_general(da, wc[pl.ds(low, Q), :], NT, preferred_element_type=jnp.float32)
-                U[h, group, :, q] = (u * q_own).astype(jnp.bfloat16).reshape(n, T, Q)
-                if theirs:
-                    rc(U.at[h, group, :, q], D.at[kk, :, q], e_s.at[kk, q], e_r.at[kk, q], partner).start()
-                return carry
-
-            lax.fori_loop(0, 2, quarter, 0)
-
-        def u_for_partner(kk):
-            for core in range(2):
-                pl.when(c == core)(functools.partial(half_u, kk, 1 - core, True))
-            for q in range(2):
-                sent.append(
-                    rc(U.at[1 - c, at(fp, OFF[kk]), :, q], D.at[kk, :, q], e_s.at[kk, q], e_r.at[kk, q], partner)
-                )
-
-        def u_for_self(kk):
-            for core in range(2):
-                pl.when(c == core)(functools.partial(half_u, kk, core, False))
+            for h in (1 - c, c):
+                rows = [(zi * (1 - h) + r * h, r * (1 - h) + yi * h) for r in range(n)]
+                half_u(rows, h, q)
+                if h is not c:
+                    piece = U.at[1 - c, at(fp, OFF[kk]), :, q]
+                    go(piece, D.at[kk, :, q], e_s.at[kk, q], e_r.at[kk, q], partner)
 
         def add_partner(kk, q):
             got(D.at[kk, :, q], e_s.at[kk, q], e_r.at[kk, q], partner)
             i = at(sp, OFF[kk])
             U[c, i, :, q] = U[c, i, :, q] + D[kk, :, q]
 
-        u_for_partner(3)
-        u_for_self(3)
-        u_for_partner(2)
         s2 = at(sp, 2)
         for d in range(2):
+            unit(3, d)
             add_partner(3, d)
             for k in (3, 2, 1, 0):
                 go(U.at[c, s2, at(fp, OFF[k]), d], RH.at[d, k], rh_s.at[d, k], rh_r.at[d, k], sdir[d])
-        u_for_self(2)
-        u_for_partner(1)
-        u_for_self(1)
-        for q in range(2):
-            add_partner(2, q)
-        for q in range(2):
-            add_partner(1, q)
+
+        def to_owner(d, k, q):
+            i, f = at(sp, 1 if d == 0 else -1), at(fp, OFF[k])
+            go(U.at[c, i, f, q], RF.at[d, k, q], rf_s.at[d, k, q], rf_r.at[d, k, q], sdir[d])
+
+        for d in range(2):
+            unit(2 - d, 1 - d)
+            add_partner(2 - d, 1 - d)
+            for k in (3, 2, 1, 0):
+                to_owner(d, k, 1 - d)
+        for d in range(2):
+            unit(2 - d, d)
+            add_partner(2 - d, d)
 
         def pass_sum(k):
             for d in range(2):
                 i, f = at(sp, 1 if d == 0 else -1), at(fp, OFF[k])
                 got(RH.at[d, k], rh_s.at[d, k], rh_r.at[d, k], sdir[d])
                 U[c, i, f, d] = U[c, i, f, d] + RH[d, k]
-                go(U.at[c, i, f], RF.at[d, k], rf_s.at[d, k], rf_r.at[d, k], sdir[d])
+                to_owner(d, k, d)
 
         pass_sum(3)
         pass_sum(2)
-        u_for_partner(0)
+        unit(0, 0)
         pass_sum(1)
         pass_sum(0)
-        u_for_self(0)
+        unit(0, 1)
         for q in range(2):
             add_partner(0, q)
 
-        def own_sum(k):
+        def own_sum(k, q):
             for d in range(2):
-                got(RF.at[d, k], rf_s.at[d, k], rf_r.at[d, k], sdir[d])
+                got(RF.at[d, k, q], rf_s.at[d, k, q], rf_r.at[d, k, q], sdir[d])
             f = at(fp, OFF[k])
-            total = U[c, sp, f].astype(jnp.float32) + RF[0, k].astype(jnp.float32)
-            U[c, sp, f] = (total + RF[1, k].astype(jnp.float32)).astype(jnp.bfloat16)
-
-        own_sum(3)
+            total = U[c, sp, f, q].astype(jnp.float32) + RF[0, k, q].astype(jnp.float32)
+            U[c, sp, f, q] = (total + RF[1, k, q].astype(jnp.float32)).astype(jnp.bfloat16)
+
         f2 = at(fp, 2)
         for d in range(2):
+            own_sum(3, d)
             go(U.at[c, sp, f2, d], RHF.at[d], hf_s.at[d], hf_r.at[d], fdir[d])
         for d, k in ((0, 2), (1, 1)):
-            own_sum(k)
             f = at(fp, OFF[k])
+            for q in range(2):
+                own_sum(k, q)
             got(RHF.at[d], hf_s.at[d], hf_r.at[d], fdir[d])
             U[c, sp, f, d] = U[c, sp, f, d] + RHF[d]
             for i, q in enumerate((1 - xl, xl)):
                 go(U.at[c, sp, f, q], RFF.at[d, q], ff2_s.at[d, i], ff2_r.at[d, i], fdir[d])
-        own_sum(0)
+        for q in range(2):
+            own_sum(0, q)
 
         def three(i, q):
             for d in range(2):
@@ -478,14 +503,19 @@
 
         values = xin[m].astype(jnp.float32)
         both = values * (dn * gain[...]) + xo[m].astype(jnp.float32) * (other * gain_o[...])
-        msend[...] = jnp.broadcast_to(jnp.sum(both, axis=-1, keepdims=True), msend.shape)
+        high = both.astype(jnp.bfloat16)
+        low = (both - high.astype(jnp.float32)).astype(jnp.bfloat16)
+        ones = jnp.ones((8, Q), jnp.bfloat16)
+        msend[:, 0:T] = lax.dot_general(
+            ones, high, NT, preferred_element_type=jnp.float32
+        ) + lax.dot_general(ones, low, NT, preferred_element_type=jnp.float32)
         for i, peer in enumerate(across):
             go(msend, mrecv.at[i], m_s.at[i], m_r.at[i], peer)
         got(RX, rx_s, rx_r, xnbr)
         gained = (dn + RX[...].astype(jnp.float32)) * gain[...]
         for i, peer in enumerate(across):
             got(mrecv.at[i], m_s.at[i], m_r.at[i], peer)
-        moment = (msend[...] + mrecv[0] + mrecv[1] + mrecv[2])[:, 0:1] / width
+        moment = ((msend[...] + mrecv[0]) + (mrecv[1] + mrecv[2])).T[0:T, 0:1] / width
         sc = info[m, z, y, :, 112:113]
         result = G[c, sp, fp, xl].astype(jnp.float32) + sc * gained - values * (sc * sc * sc * moment)
         out[m] = result.astype(jnp.bfloat16)
@@ -520,12 +550,9 @@
     router = router_w[0]
     experts = router.shape[1]
     width = w_gate.shape[1]
-    gain_full = norm_gain.astype(jnp.float32)
     turned = jnp.pad(router.T, ((0, 16 - experts), (0, 0)))
     rows = jnp.swapaxes(routes[0], 1, 2).astype(jnp.float32)
     rows = jnp.pad(rows, ((0, 0), (0, 6), (0, lanes - T)), constant_values=-5.0)
-    spaced = jnp.pad(router[:, :, None], ((0, 0), (0, 0), (0, 15))).reshape(Q, experts * 16)
-    rp = jnp.pad(spaced, ((0, 0), (48, lanes - 48 - experts * 16)))
 
     bf, f32 = jnp.bfloat16, jnp.float32
     vm = pl.BlockSpec(memory_space=pltpu.VMEM)
@@ -535,7 +562,7 @@
     grads = pl.pallas_call(
         functools.partial(kernel, sections, n, (micros, T, Q, F, cap, lanes)),
         out_shape=jax.ShapeDtypeStruct((micros, T, Q), bf),
-        in_specs=[vm] * 5 + [anym] * 6,
+        in_specs=[vm] * 5 + [anym] * 5,
         out_specs=vm,
         scratch_shapes=[
             pltpu.VMEM((2, n, n, 2, T, Q), bf),
@@ -547,8 +574,8 @@
             pltpu.VMEM((2, 2, T, Q), bf),
             pltpu.VMEM((T, Q), bf),
             pltpu.VMEM((micros, T, Q), bf),
-            pltpu.VMEM((3, T, lanes), f32),
-            pltpu.VMEM((T, lanes), f32),
+            pltpu.VMEM((3, 8, lanes), f32),
+            pltpu.VMEM((8, lanes), f32),
             pltpu.VMEM((n, n, T, F), f32),
             pltpu.VMEM((n, n, T, F), f32),
             pltpu.VMEM((n, n, T, F), f32),
@@ -561,6 +588,8 @@
             pltpu.VMEM((n * n, cap, F), bf),
             pltpu.VMEM((micros, T, Q), bf),
             pltpu.VMEM((1, Q), f32),
+            pltpu.VMEM((1, Q), f32),
+            pltpu.VMEM((Q, lanes), bf),
             pltpu.VMEM((micros, 8, lanes), f32),
             pltpu.VMEM((3, micros, 8, lanes), f32),
             pltpu.VMEM((micros, 8, lanes), f32),
@@ -569,9 +598,9 @@
             dma((6,)),
             dma, dma,
             dma((2, 2)), dma((2, 2)), dma((2,)), dma((2,)),
-            dma((2, 2)), dma((2, 2)), dma((4, 2)), dma((4, 2)), dma((4, 2)), dma((4, 2)),
+            dma((4, 2, 2)), dma((4, 2, 2)), dma((4, 2)), dma((4, 2)),
             dma((4, 4)), dma((4, 4)),
-            dma((4, 2)), dma((4, 2)), dma((2, 4)), dma((2, 4)), dma((2, 4)), dma((2, 4)),
+            dma((4, 2)), dma((4, 2)), dma((2, 4)), dma((2, 4)), dma((2, 4, 2)), dma((2, 4, 2)),
             dma((2,)), dma((2,)), dma((2, 2)), dma((2, 2)), dma, dma,
             dma((3,)), dma((3,)), dma((micros,)), dma((micros,)),
             dma, dma, dma, dma, dma((3,)), dma((3,)), dma((3,)), dma((3,)),
@@ -583,8 +612,8 @@
         ),
         name="layer_back",
     )(
-        grad_out, layer_inputs[0], gain_full, turned, rows, saved_gate[0], saved_up[0],
-        w_down[0], w_gate[0], w_up[0], rp,
+        grad_out, layer_inputs[0], norm_gain, turned, rows, saved_gate[0], saved_up[0],
+        w_down[0], w_gate[0], w_up[0],
     )
     return grads[None]
 

time: 224 us -> 215 us (0.960)
  Pallas kernels: 217 us -> 211 us
    pallas_call x1, Pallas kernels: 217 us -> 211 us  [on_device(): pl.pallas_call(functools.partial(kernel, sections, n, (micros, T, Q, F, c...]
where the time goes in v4:
time: 215 us
  Pallas kernels  211 us (98%)
  local copies, waits for them, and re-layouts  3.56 us (2%)
    pallas_call x1, Pallas kernels, on_device(): pl.pallas_call(functools.partial(kernel, sections, n, (micros, T, Q, F, c...  211 us

profile of v4, /device:TPU:1, one launch (start us, length us, event | category | flops | bytes accessed | tf_op | source)
XLA Modules:
  0.0 215.3 jit_solution(9334621130140624538)
XLA Ops:
  0.0 0.7 convert_bitcast_fusion
  0.7 0.6 pad.9.rows_in
  1.3 1.3 pad.8.rt_in
  2.6 211.0 %layer_back.1 = bf16[2,80,768]{2,1,0:T(8,128)(2,1)} custom-call(bf16[2,80,768]{2,1,0:T(8,128)(2,1)} %gout.1, bf16[2,80,768]{2,1,0:T(8,128)(2,1)} %bitcast.20, bf16[1,768]{1,0:T(2,128)(2,1)} %gain_in.1, bf16[16,768]{1,0:T(8,128)(2,1)} %pad.8.rt_in, f32[2,8,128]{2,1,0:T(8,128)} %pad.9.rows_in, bf16[2,16,64,512]{3,2,1,0:T(8,128)(2,1)} %bitcast.17, ...), custom_call_target="tpu_custom_call" | custom-call | tf_op jit(solution)/shard_map/layer_back/pallas_call | solution.py:562
  213.6 1.7 copy.12
